TPU v7x, 32 devices: a whole 2x2x4 slice. The times are simulated.
32 devices in a mesh: groups: 1, blk: 16 (over z, y, x), head: 2 (over core).
Axes of the slice: x: 2, y: 2, z: 4, core: 2. Of those that a mesh axis runs over, the one named last changes fastest.
Arguments:
- queries: bfloat16 [128, 8192], P(('groups', 'blk'), 'head'), may hold values from -6 to 6
- key_cache: bfloat16 [2, 32768, 8, 128], P('groups', 'blk', 'head'), may hold values from -18 to 18
- value_cache: bfloat16 [2, 32768, 8, 128], P('groups', 'blk', 'head'), may hold values from -6 to 6
- lengths: int32 [2], P('groups'), may hold values from 0 to 32704
- residual: bfloat16 [128, 8192], P('groups', 'blk'), may hold values from -6 to 6
- out_weight: bfloat16 [8192, 8192], P('head', 'blk'), may hold values from -0.0625 to 0.0625
- norm_gain: bfloat16 [8192], P('blk'), may hold values from 0.099609375 to 1.8984375
- gate_weight: bfloat16 [8192, 16384], P(None, ('head', 'blk')), may hold values from -0.0625 to 0.0625
- up_weight: bfloat16 [8192, 16384], P(None, ('head', 'blk')), may hold values from -0.0625 to 0.0625
- down_weight: bfloat16 [16384, 8192], P('head', 'blk'), may hold values from -0.046875 to 0.046875
Outputs:
- layer_out: bfloat16 [128, 8192], P('groups', 'blk')
Inputs may be any that keep to these rules, and one draw needn't show every extreme that they name: lengths[b] + 64 <= 32768; the cache holds sequence b's new keys and values at positions lengths[b] to lengths[b] + 63.
All inputs are finite; a program needn't handle non-finite values.
Results may differ from a plain program's by a relative error of at most 0.01.
Values may be sent and summed in bfloat16 or wider, within the bound.
No kernel may reach another device: no remote copies, remote signals or barrier semaphores. Data moves between devices by JAX's collectives and lax.ppermute only.
A program may use at most 128 MiB of HBM per device.

v0:
```python
import functools

import jax
import jax.numpy as jnp
from jax import lax
from jax.experimental import pallas as pl
from jax.experimental.pallas import tpu as pltpu
from jax.sharding import PartitionSpec as P

neg_big = -1e30
epsilon = 1e-06
LANES = 128
bf16 = jnp.bfloat16
f32 = jnp.float32


def xor_blk(x, mask, blocks):
    return lax.ppermute(x, "blk", [(i, i ^ mask) for i in range(blocks)])


def swap_head(x):
    n = lax.axis_size("head")
    return lax.ppermute(x, "head", [(i, n - 1 - i) for i in range(n)])


def far_parts(x, near, far, blocks):
    return [x] + [xor_blk(x, f * near, blocks) for f in range(1, far)]


def near_parts(own, near, blocks):
    return [own] + [xor_blk(own, p, blocks) for p in range(1, near)]


def gather(x, near, far, blocks, join):
    return near_parts(join(far_parts(x, near, far, blocks)), near, blocks)


def gather_halves(first, second, near, far, blocks, join):
    one = [join(far_parts(first, near, far, blocks))]
    two = [join(far_parts(second, near, far, blocks))]
    for p in range(1, near):
        low, high = p & -p, 1 << (p.bit_length() - 1)
        one.append(xor_blk(one[p ^ low], low, blocks))
        two.append(xor_blk(two[p ^ high], high, blocks))
    return list(zip(one, two))


def split3(v):
    hi = v.astype(bf16).astype(f32)
    mid = (v - hi).astype(bf16).astype(f32)
    low = (v - hi - mid).astype(bf16).astype(f32)
    return hi, mid, low


def attention(qs, parts, keys, values, scalars, near, far, batch, new_tokens, heads_local):
    rows, width = qs[0].shape
    kv_local, ctx_dev, head_dim = keys.shape[1:]
    group = heads_local // kv_local
    slot_rows = rows // batch
    rows_dev = rows // far
    count = len(parts)
    log2e = 1.4426950408889634
    scale = head_dim ** (-0.5) * log2e
    tile = min(512, ctx_dev)
    tiles = ctx_dev // tile
    chunk_m = group * slot_rows
    m_rows = count * chunk_m
    units = batch * kv_local

    def kernel(s_ref, *refs):
        q_refs, k_hbm, v_hbm, o_refs = refs[:count], refs[count], refs[count + 1], refs[count + 2 : -6]
        k_all, v_all, room, best, scores, sems = refs[-6:]
        me = s_ref[0]

        def copies(u, which=(0, 1)):
            slot, g = u // kv_local, u % kv_local
            seq = s_ref[1] ^ slot
            picks = ((k_hbm, k_all), (v_hbm, v_all))
            return [
                pltpu.make_async_copy(picks[i][0].at[seq, g], picks[i][1].at[u], sems.at[u, i]) for i in which
            ]

        for u in range(4):
            for c in copies(u):
                c.start()
        row = lax.broadcasted_iota(jnp.int32, (chunk_m, LANES), 0) % slot_rows
        lanes = lax.broadcasted_iota(jnp.int32, (chunk_m, LANES), 1)
        piece = row // rows_dev
        for slot in range(batch):
            length = s_ref[2 + (s_ref[1] ^ slot)]
            for c, part in enumerate(parts):
                first = jnp.zeros((chunk_m, LANES), jnp.int32)
                for p in range(far // batch):
                    mask = (slot * (far // batch) + p) * near + part
                    start = ((me ^ mask) * rows_dev) % new_tokens
                    first = jnp.where(piece == p, start, first)
                limit = first + row % rows_dev + length - me * ctx_dev
                room[slot, c * chunk_m : (c + 1) * chunk_m, :] = limit - lanes

        def whole(u):
            return s_ref[2 + (s_ref[1] ^ (u // kv_local))] - me * ctx_dev >= ctx_dev - 1

        def produce(u, parity, masked):
            slot, g = u // kv_local, u % kv_local
            own_rows = pl.ds(pl.multiple_of(slot * slot_rows, slot_rows), slot_rows)
            lhs = jnp.concatenate(
                [
                    q[own_rows, pl.ds(pl.multiple_of((g * group + j) * head_dim, head_dim), head_dim)]
                    for q in q_refs
                    for j in range(group)
                ],
                axis=0,
            )
            copies(u, (0,))[0].wait()
            high = jnp.full((m_rows, LANES), neg_big, f32)
            for t in range(tiles):
                s = lax.dot_general(
                    lhs,
                    k_all[u, t * tile : (t + 1) * tile, :],
                    (((1,), (1,)), ((), ())),
                    preferred_element_type=f32,
                )
                for i in range(0, tile, LANES):
                    part = s[:, i : i + LANES]
                    if masked:
                        part = jnp.where(room[slot] >= t * tile + i, part, neg_big)
                    scores[parity, :, t * tile + i : t * tile + i + LANES] = part
                    high = jnp.maximum(high, part)
                yield
            best[parity] = high

        def consume(u, parity):
            slot, g = u // kv_local, u % kv_local
            own_rows = pl.ds(pl.multiple_of(slot * slot_rows, slot_rows), slot_rows)
            top = jnp.max(best[parity], axis=1, keepdims=True)
            copies(u, (1,))[0].wait()
            total = jnp.zeros((m_rows, LANES), f32)
            acc = jnp.zeros((m_rows, head_dim), f32)
            for t in range(tiles):
                w = jnp.exp2((scores[parity, :, t * tile : (t + 1) * tile] - top) * scale)
                for i in range(0, tile, LANES):
                    total += w[:, i : i + LANES]
                acc += jnp.dot(w.astype(bf16), v_all[u, t * tile : (t + 1) * tile, :], preferred_element_type=f32)
                yield
            total = jnp.sum(total, axis=1, keepdims=True)
            seen = top > 0.5 * neg_big
            mean = acc * jnp.where(seen, 1.0 / total, 0.0)
            lse = jnp.where(seen, top * (scale / log2e) + jnp.log(total), neg_big)
            lane = lax.broadcasted_iota(jnp.int32, (slot_rows, LANES), 1)
            for c in range(count):
                stats = o_refs[c][own_rows, width:].astype(f32)
                for j in range(group):
                    block = slice(c * chunk_m + j * slot_rows, c * chunk_m + (j + 1) * slot_rows)
                    head = g * group + j
                    at = pl.ds(pl.multiple_of(head * head_dim, head_dim), head_dim)
                    o_refs[c][own_rows, at] = mean[block].astype(bf16)
                    for i, v in enumerate(split3(lse[block])):
                        stats = jnp.where(lane == i * heads_local + head, v, stats)
                o_refs[c][own_rows, width:] = stats.astype(bf16)

        for o in o_refs:
            o[:, width:] = jnp.zeros((rows, LANES), bf16)

        @pl.when(whole(0))
        def _():
            for _ in produce(0, 0, False):
                pass

        @pl.when(jnp.logical_not(whole(0)))
        def _():
            for _ in produce(0, 0, True):
                pass

        def step(u, nothing):
            @pl.when(u + 4 < units)
            def _():
                for c in copies(u + 4):
                    c.start()

            def both(masked):
                ahead, now = produce(u + 1, (u + 1) % 2, masked), consume(u, u % 2)
                for _ in range(tiles + 1):
                    next(now, None)
                    next(ahead, None)

            @pl.when(whole(u + 1))
            def _():
                both(False)

            @pl.when(jnp.logical_not(whole(u + 1)))
            def _():
                both(True)

            return nothing

        lax.fori_loop(0, units - 1, step, 0)
        for _ in consume(units - 1, (units - 1) % 2):
            pass

    return pl.pallas_call(
        kernel,
        grid_spec=pltpu.PrefetchScalarGridSpec(
            num_scalar_prefetch=1,
            grid=(1,),
            in_specs=[pl.BlockSpec((rows, width), lambda i, s: (0, 0))] * count
            + [pl.BlockSpec(memory_space=pltpu.HBM)] * 2,
            out_specs=[pl.BlockSpec((rows, width + LANES), lambda i, s: (0, 0))] * count,
            scratch_shapes=[
                pltpu.VMEM((units, ctx_dev, head_dim), bf16),
                pltpu.VMEM((units, ctx_dev, head_dim), bf16),
                pltpu.VMEM((batch, m_rows, LANES), jnp.int32),
                pltpu.VMEM((2, m_rows, LANES), f32),
                pltpu.VMEM((2, m_rows, ctx_dev), f32),
                pltpu.SemaphoreType.DMA((units, 2)),
            ],
        ),
        out_shape=[jax.ShapeDtypeStruct((rows, width + LANES), bf16)] * count,
        compiler_params=pltpu.CompilerParams(vmem_limit_bytes=40 << 20),
        cost_estimate=pl.CostEstimate(
            flops=8 * count * rows * width * ctx_dev,
            bytes_accessed=4 * keys.size,
            transcendentals=count * rows * heads_local * ctx_dev,
        ),
    )(scalars, *qs, keys, values)


def merge(parts, heads_local, head_dim, last):
    rows = parts[0].shape[0]
    width = heads_local * head_dim
    count = len(parts)

    def kernel(*refs):
        ins, out = refs[:count], refs[count]
        lses = []
        for r in ins:
            s = r[:, width:].astype(f32)
            lses.append(
                s + pltpu.roll(s, LANES - heads_local, 1) + pltpu.roll(s, LANES - 2 * heads_local, 1)
            )
        top = functools.reduce(jnp.maximum, lses)
        ws = [jnp.exp(v - top) for v in lses]
        total = functools.reduce(jnp.add, ws)
        ws = [w / total for w in ws]
        for j in range(heads_local):
            cols = slice(j * head_dim, (j + 1) * head_dim)
            acc = sum(w[:, j : j + 1] * r[:, cols].astype(f32) for w, r in zip(ws, ins))
            out[:, cols] = acc.astype(bf16)
        if not last:
            lane = lax.broadcasted_iota(jnp.int32, (rows, LANES), 1)
            hi, mid, low = (
                jnp.where(lane < heads_local, v, 0.0) for v in split3(jnp.where(lane < heads_local, top + jnp.log(total), 0.0))
            )
            out[:, width:] = (
                hi + pltpu.roll(mid, heads_local, 1) + pltpu.roll(low, 2 * heads_local, 1)
            ).astype(bf16)

    return pl.pallas_call(
        kernel,
        out_shape=jax.ShapeDtypeStruct((rows, width if last else width + LANES), bf16),
        compiler_params=pltpu.CompilerParams(vmem_limit_bytes=16 << 20),
        cost_estimate=pl.CostEstimate(flops=rows * width * 1000, bytes_accessed=rows * width * 10, transcendentals=0),
    )(*parts)


def out_projection(chunks, weight, scalars, near, far, rows_dev):
    count = len(chunks)
    chunk_rows = chunks[0].shape[0]
    rows = count * chunk_rows
    depth, columns = weight.shape
    step = min(1024, depth)
    steps = depth // step

    def kernel(s_ref, *refs):
        ins, w_hbm, o_ref, w_all, sems = refs[:count], refs[count], refs[count + 1], refs[count + 2], refs[count + 3]
        copies = [
            pltpu.make_async_copy(w_hbm.at[pl.ds(k * step, step)], w_all.at[k], sems.at[k]) for k in range(steps)
        ]
        for c in copies:
            c.start()
        there = lax.broadcasted_iota(jnp.int32, (rows, rows), 0)
        here = lax.broadcasted_iota(jnp.int32, (rows, rows), 1)
        piece = here // rows_dev
        mask = (piece % far) * near + piece // far
        goal = (mask ^ s_ref[0]) * rows_dev + here % rows_dev
        order = jnp.where(goal == there, 1.0, 0.0).astype(bf16)
        acc = jnp.zeros((rows, columns), f32)
        for k in range(steps):
            rel = jnp.concatenate([r[:, k * step : (k + 1) * step] for r in ins], axis=0)
            lhs = jnp.dot(order, rel, preferred_element_type=f32).astype(bf16)
            copies[k].wait()
            acc += jnp.dot(lhs, w_all[k], preferred_element_type=f32)
        o_ref[...] = acc.astype(bf16)

    return pl.pallas_call(
        kernel,
        grid_spec=pltpu.PrefetchScalarGridSpec(
            num_scalar_prefetch=1,
            grid=(1,),
            in_specs=[pl.BlockSpec((chunk_rows, depth), lambda k, s: (0, 0))] * count
            + [pl.BlockSpec(memory_space=pltpu.HBM)],
            out_specs=pl.BlockSpec((rows, columns), lambda k, s: (0, 0)),
            scratch_shapes=[pltpu.VMEM((steps, step, columns), bf16), pltpu.SemaphoreType.DMA((steps,))],
        ),
        out_shape=jax.ShapeDtypeStruct((rows, columns), bf16),
        compiler_params=pltpu.CompilerParams(vmem_limit_bytes=24 << 20),
        cost_estimate=pl.CostEstimate(flops=2 * rows * depth * columns, bytes_accessed=2 * weight.size, transcendentals=0),
        name="out_projection",
    )(scalars, *chunks, weight)


STAT_ROWS = 8


def stream_step(residual, mine, other, gain, scalars):
    rows, columns = residual.shape
    half = rows // 2

    def kernel(s_ref, r_ref, a_ref, b_ref, g_ref, stream_ref, send_ref):
        core = s_ref[0]
        stream_ref[...] = r_ref[...].astype(f32) + (a_ref[...].astype(f32) + b_ref[...].astype(f32))
        own = stream_ref[pl.ds(pl.multiple_of(core * half, half), half), :]
        send_ref[:half, :] = (own * g_ref[...].astype(f32)).astype(bf16)
        squares = jnp.sum(own * own, axis=1, keepdims=True)
        i = lax.broadcasted_iota(jnp.int32, (half, columns), 0)
        j = lax.broadcasted_iota(jnp.int32, (half, columns), 1)
        line = jnp.sum(jnp.where(i == j, squares, 0.0), axis=0, keepdims=True)
        row = lax.broadcasted_iota(jnp.int32, (STAT_ROWS, columns), 0)
        stats = jnp.zeros((STAT_ROWS, columns), f32)
        for n, v in enumerate(split3(line)):
            stats = jnp.where(row == n, v, stats)
        send_ref[half:, :] = stats.astype(bf16)

    return pl.pallas_call(
        kernel,
        grid_spec=pltpu.PrefetchScalarGridSpec(
            num_scalar_prefetch=1,
            grid=(1,),
            in_specs=[pl.BlockSpec((rows, columns), lambda i, s: (0, 0))] * 3
            + [pl.BlockSpec((1, columns), lambda i, s: (0, 0))],
            out_specs=[
                pl.BlockSpec((rows, columns), lambda i, s: (0, 0)),
                pl.BlockSpec((half + STAT_ROWS, columns), lambda i, s: (0, 0)),
            ],
        ),
        out_shape=[
            jax.ShapeDtypeStruct((rows, columns), f32),
            jax.ShapeDtypeStruct((half + STAT_ROWS, columns), bf16),
        ],
        compiler_params=pltpu.CompilerParams(vmem_limit_bytes=16 << 20),
        name="stream_step",
    )(scalars, residual, mine, other, gain)


def feed_chunk(own, other, gate_weight, up_weight, scalars, carry, part, near, far, width, last):
    half = own.shape[1] - STAT_ROWS
    columns = own.shape[2]
    units = gate_weight.shape[1]
    rows = 2 * half

    def kernel(s_ref, a_ref, b_ref, gw_hbm, uw_hbm, *rest):
        g_all, u_all, sems = rest[-3:]
        rest = rest[:-3]
        copies = []
        for k in range(far):
            at = pl.ds(pl.multiple_of((s_ref[0] ^ (k * near + part)) * columns, columns), columns)
            copies.append(
                (
                    pltpu.make_async_copy(gw_hbm.at[at], g_all.at[k], sems.at[k, 0]),
                    pltpu.make_async_copy(uw_hbm.at[at], u_all.at[k], sems.at[k, 1]),
                )
            )
        for pair in copies:
            for c in pair:
                c.start()
        upper = s_ref[1] == 0
        if carry is None:
            gate = jnp.zeros((rows, units), f32)
            up = jnp.zeros((rows, units), f32)
            top = jnp.zeros((1, LANES), f32)
            low = jnp.zeros((1, LANES), f32)
        else:
            gi_ref, ui_ref, si_ref = rest[:3]
            rest = rest[3:]
            gate, up = gi_ref[...], ui_ref[...]
            top, low = si_ref[0:1, :], si_ref[1:2, :]
        for k in range(far):
            mine, theirs = a_ref[k].astype(f32), b_ref[k].astype(f32)
            lhs = jnp.concatenate(
                [
                    jnp.where(upper, mine[:half], theirs[:half]),
                    jnp.where(upper, theirs[:half], mine[:half]),
                ],
                axis=0,
            ).astype(bf16)
            m = jnp.sum(mine[half:], axis=0, keepdims=True)[:, :LANES]
            t = jnp.sum(theirs[half:], axis=0, keepdims=True)[:, :LANES]
            top += jnp.where(upper, m, t)
            low += jnp.where(upper, t, m)
            for c in copies[k]:
                c.wait()
            gate += jnp.dot(lhs, g_all[k], preferred_element_type=f32)
            up += jnp.dot(lhs, u_all[k], preferred_element_type=f32)
        if not last:
            g_ref, u_ref, q_ref = rest
            g_ref[...] = gate
            u_ref[...] = up
            row = lax.broadcasted_iota(jnp.int32, (8, LANES), 0)
            q_ref[...] = jnp.where(row == 0, top, jnp.where(row == 1, low, 0.0))
            return
        i = lax.broadcasted_iota(jnp.int32, (half, LANES), 0)
        j = lax.broadcasted_iota(jnp.int32, (half, LANES), 1)
        for n, line in enumerate((top, low)):
            column = jnp.sum(jnp.where(i == j, line, 0.0), axis=1, keepdims=True)
            r = lax.rsqrt(column / width + epsilon)
            g = gate[n * half : (n + 1) * half] * r
            u = up[n * half : (n + 1) * half] * r
            rest[n][...] = (g / (1.0 + jnp.exp(-g)) * u).astype(bf16)

    flat = lambda shape: pl.BlockSpec(shape, lambda i, s: (0,) * len(shape))
    acc_shapes = [(rows, units), (rows, units), (8, LANES)]
    return pl.pallas_call(
        kernel,
        grid_spec=pltpu.PrefetchScalarGridSpec(
            num_scalar_prefetch=1,
            grid=(1,),
            in_specs=[flat(own.shape), flat(own.shape)]
            + [pl.BlockSpec(memory_space=pltpu.HBM)] * 2
            + ([flat(x) for x in acc_shapes] if carry is not None else []),
            out_specs=[flat((half, units))] * 2 if last else [flat(x) for x in acc_shapes],
            scratch_shapes=[
                pltpu.VMEM((far, columns, units), bf16),
                pltpu.VMEM((far, columns, units), bf16),
                pltpu.SemaphoreType.DMA((far, 2)),
            ],
        ),
        out_shape=[jax.ShapeDtypeStruct((half, units), bf16)] * 2
        if last
        else [jax.ShapeDtypeStruct(x, f32) for x in acc_shapes],
        compiler_params=pltpu.CompilerParams(vmem_limit_bytes=20 << 20),
        cost_estimate=pl.CostEstimate(
            flops=4 * rows * far * columns * units, bytes_accessed=4 * far * columns * units, transcendentals=0
        ),
    )(scalars, own, other, gate_weight, up_weight, *(carry or ()))


def down_chunk(halves, weight, scalars, carry, part, near, far, last):
    _, half, units = halves[0].shape
    rows = half * len(halves)
    columns = weight.shape[1]

    def kernel(s_ref, *refs):
        h_refs, w_hbm, rest = refs[: len(halves)], refs[len(halves)], refs[len(halves) + 1 :]
        w_all, sems = rest[-2:]
        copies = []
        for k in range(far):
            at = pl.ds(pl.multiple_of((s_ref[0] ^ (k * near + part)) * units, units), units)
            copies.append(pltpu.make_async_copy(w_hbm.at[at], w_all.at[k], sems.at[k]))
        for c in copies:
            c.start()
        acc = jnp.zeros((rows, columns), f32) if carry is None else rest[0][...]
        for k in range(far):
            lhs = jnp.concatenate([h[k] for h in h_refs], axis=0)
            copies[k].wait()
            acc += jnp.dot(lhs, w_all[k], preferred_element_type=f32)
        rest[-3][...] = acc.astype(rest[-3].dtype)

    flat = lambda shape: pl.BlockSpec(shape, lambda i, s: (0,) * len(shape))
    return pl.pallas_call(
        kernel,
        grid_spec=pltpu.PrefetchScalarGridSpec(
            num_scalar_prefetch=1,
            grid=(1,),
            in_specs=[flat(h.shape) for h in halves]
            + [pl.BlockSpec(memory_space=pltpu.HBM)]
            + ([flat((rows, columns))] if carry is not None else []),
            out_specs=flat((rows, columns)),
            scratch_shapes=[pltpu.VMEM((far, units, columns), bf16), pltpu.SemaphoreType.DMA((far,))],
        ),
        out_shape=jax.ShapeDtypeStruct((rows, columns), bf16 if last else f32),
        compiler_params=pltpu.CompilerParams(vmem_limit_bytes=20 << 20),
        cost_estimate=pl.CostEstimate(
            flops=2 * rows * far * columns * units, bytes_accessed=2 * far * columns * units, transcendentals=0
        ),
    )(scalars, *halves, weight, *(() if carry is None else (carry,)))


def body(
    queries,
    key_cache,
    value_cache,
    lengths,
    residual,
    out_weight,
    norm_gain,
    gate_weight,
    up_weight,
    down_weight,
):
    blocks = lax.axis_size("blk")
    me = lax.axis_index("blk").astype(jnp.int32)
    core = lax.axis_index("head").astype(jnp.int32)
    batch, _, _, head_dim = key_cache.shape
    rows_dev, width_local = queries.shape
    heads_local = width_local // head_dim
    new_tokens = rows_dev * blocks // batch
    near = 1 << ((blocks.bit_length() - 1) // 2)
    far = blocks // near
    width = residual.shape[1] * blocks

    scalars = jnp.concatenate([jnp.stack([me, me // (blocks // batch)]), lengths])
    spot = jnp.stack([me, core])
    rows_join = lambda parts: jnp.concatenate(parts, axis=0)
    stack_join = lambda parts: jnp.stack(parts, axis=0)

    stay = lambda x: pltpu.with_memory_space_constraint(x, pltpu.HBM)
    out_weight, gate_weight, up_weight, down_weight = map(
        stay, (out_weight, gate_weight, up_weight, down_weight)
    )
    keys = stay(jnp.transpose(key_cache, (0, 2, 1, 3)))
    values = stay(jnp.transpose(value_cache, (0, 2, 1, 3)))
    asked = gather(queries, near, far, blocks, rows_join)
    partial = []
    for group in [[0], list(range(1, near - 1)), [near - 1]]:
        outs = attention(
            [asked[p] for p in group], group, keys, values, scalars, near, far, batch, new_tokens, heads_local
        )
        partial += [o if p == 0 else xor_blk(o, p, blocks) for p, o in zip(group, outs)]
    plane = merge(partial, heads_local, head_dim, False)
    pieces = [plane[f * rows_dev : (f + 1) * rows_dev] for f in range(far)]
    pieces = [pieces[0]] + [xor_blk(pieces[f], f * near, blocks) for f in range(1, far)]
    attn = merge(pieces, heads_local, head_dim, True)

    mine = out_projection(gather(attn, near, far, blocks, rows_join), out_weight, scalars, near, far, rows_dev)
    stream, send = stream_step(residual, mine, swap_head(mine), norm_gain[None, :], core[None])

    normed = gather(send, near, far, blocks, stack_join)
    carry = None
    for p in range(near):
        other = swap_head(normed[p])
        carry = feed_chunk(normed[p], other, gate_weight, up_weight, spot, carry, p, near, far, width, p == near - 1)
    hidden = gather_halves(*carry, near, far, blocks, stack_join)
    carry = None
    for p in range(near):
        carry = down_chunk(hidden[p], down_weight, spot, carry, p, near, far, p == near - 1)
    total = carry.astype(f32) + swap_head(carry).astype(f32)
    return (stream + total).astype(bf16)


def solution(mesh):
    in_specs = (
        P(("groups", "blk"), "head"),
        P("groups", "blk", "head", None),
        P("groups", "blk", "head", None),
        P("groups"),
        P("groups", "blk"),
        P("head", "blk"),
        P("blk"),
        P(None, ("head", "blk")),
        P(None, ("head", "blk")),
        P("head", "blk"),
    )
    out_specs = P("groups", "blk")

    return jax.shard_map(body, mesh=mesh, in_specs=in_specs, out_specs=out_specs, check_vma=False)
```

profile of v0, /device:TPU:0, one launch (start us, length us, event | category | flops | bytes accessed | tf_op | source)
XLA Modules:
  0.0 162.4 jit_solution(16003665698862709163)
XLA Ops:
  0.0 3.1 %collective-permute-start = (bf16[8,4096]{1,0:T(8,128)(2,1)}, bf16[8,4096]{1,0:T(8,128)(2,1)S(1)}, u32[]{:S(2)}, u32[]{:S(2)}) collective-permute-start(bf16[8,4096]{1,0:T(8,128)(2,1)} %param.10), channel_id=1, source_target_pairs={{0,8},{2,10},{4,12},{6,14},{8,0},{10,2},{12,4},{14,6},{16,24},{18,... | collective-permute-start | bytes 196616 | tf_op jit(solution)/shard_map/ppermute | solution.py:18
  3.1 2.6 %collective-permute-start.1 = (bf16[8,4096]{1,0:T(8,128)(2,1)}, bf16[8,4096]{1,0:T(8,128)(2,1)S(1)}, u32[]{:S(2)}, u32[]{:S(2)}) collective-permute-start(bf16[8,4096]{1,0:T(8,128)(2,1)} %param.10), channel_id=1, source_target_pairs={{0,16},{2,18},{4,20},{6,22},{8,24},{10,26},{12,28},{14,30},{16,0},... | collective-permute-start | bytes 196616 | tf_op jit(solution)/shard_map/ppermute | solution.py:18
  6.6 4.0 %collective-permute-done.1 = bf16[8,4096]{1,0:T(8,128)(2,1)S(1)} collective-permute-done((bf16[8,4096]{1,0:T(8,128)(2,1)}, bf16[8,4096]{1,0:T(8,128)(2,1)S(1)}, u32[]{:S(2)}, u32[]{:S(2)}) %collective-permute-start.1) | collective-permute-done | bytes 65568 | tf_op jit(solution)/shard_map/ppermute | solution.py:18
  15.0 6.6 %copy_bitcast_fusion = (bf16[2,4,2048,128]{3,2,1,0:T(8,128)(2,1)}, bf16[2,4,2048,128]{3,2,1,0:T(8,128)(2,1)}) fusion(bf16[2,2048,4,128]{3,2,1,0:T(4,128)(2,1)} %param.12, bf16[2,2048,4,128]{3,2,1,0:T(4,128)(2,1)} %param.11), kind=kLoop, calls=%fused_computation | loop fusion | bytes 16777216 | tf_op jit(solution)/shard_map/transpose | solution.py:520
  22.2 10.8 %shard_map.101 = (bf16[32,4224]{1,0:T(8,128)(2,1)S(1)}, bf16[32,4224]{1,0:T(8,128)(2,1)S(1)}) custom-call(s32[4]{0:T(128)S(1)} %pad_add_fusion.s_ref, bf16[32,4096]{1,0:T(8,128)(2,1)S(1)} %collective-permute-done.3.refs_0_, bf16[32,4096]{1,0:T(8,128)(2,1)S(1)} %collective-permute-done.4.refs_1_, bf16[2,4,2048,128]{3,2,1,0:T(8,128)(2,1)} %get-tuple-element.40.refs_1_.refs_2_, ...), custom_call_target="tpu_custom_call" | custom-call | flops 4294967296 | bytes 8388608 | tf_op jit(solution)/shard_map/pallas_call | solution.py:200
  36.3 7.6 %shard_map.102 = bf16[32,4224]{1,0:T(8,128)(2,1)S(1)} custom-call(s32[4]{0:T(128)S(1)} %pad_add_fusion.s_ref, bf16[32,4096]{1,0:T(8,128)(2,1)S(1)} %collective-permute-done.7.refs_0_, bf16[2,4,2048,128]{3,2,1,0:T(8,128)(2,1)} %get-tuple-element.40.refs_1_.refs_2_, bf16[2,4,2048,128]{3,2,1,0:T(8,128)(2,1)} %get-tuple-element.39.refs_2_.refs_3_), custom_call_target="tpu_custom_call" | custom-call | flops 2147483648 | bytes 8388608 | tf_op jit(solution)/shard_map/pallas_call | solution.py:200
  44.2 7.8 %shard_map.100.refs_0_ = bf16[32,4224]{1,0:T(8,128)(2,1)S(1)} custom-call(s32[4]{0:T(128)S(1)} %pad_add_fusion.s_ref, bf16[32,4096]{1,0:T(8,128)(2,1)S(1)} %constant_dynamic-update-slice_fusion.refs_0_, bf16[2,4,2048,128]{3,2,1,0:T(8,128)(2,1)} %get-tuple-element.40.refs_1_.refs_2_, bf16[2,4,2048,128]{3,2,1,0:T(8,128)(2,1)} %get-tuple-element.39.refs_2_.refs_3_), custom_call_target="tpu_custom_call" | custom-call | flops 2147483648 | bytes 8388608 | tf_op jit(solution)/shard_map/pallas_call | solution.py:200
  52.9 2.1 %collective-permute-start.10 = (bf16[8,4224]{1,0:T(8,128)(2,1)S(1)}, bf16[8,4224]{1,0:T(8,128)(2,1)S(1)}, u32[]{:S(2)}, u32[]{:S(2)}) collective-permute-start(bf16[8,4224]{1,0:T(8,128)(2,1)S(1)} %get-tuple-element.36), channel_id=1, source_target_pairs={{0,16},{2,18},{4,20},{6,22},{8,24},{10,26},{12,28},{14,30},{16,0},... | collective-permute-start | bytes 202760 | tf_op jit(solution)/shard_map/ppermute | solution.py:18
  56.4 2.3 %collective-permute-done.10.refs_2_ = bf16[8,4224]{1,0:T(8,128)(2,1)S(1)} collective-permute-done((bf16[8,4224]{1,0:T(8,128)(2,1)S(1)}, bf16[8,4224]{1,0:T(8,128)(2,1)S(1)}, u32[]{:S(2)}, u32[]{:S(2)}) %collective-permute-start.10) | collective-permute-done | bytes 67616 | tf_op jit(solution)/shard_map/ppermute | solution.py:18
  58.7 2.7 %collective-permute-done.11.refs_3_ = bf16[8,4224]{1,0:T(8,128)(2,1)S(1)} collective-permute-done((bf16[8,4224]{1,0:T(8,128)(2,1)S(1)}, bf16[8,4224]{1,0:T(8,128)(2,1)S(1)}, u32[]{:S(2)}, u32[]{:S(2)}) %collective-permute-start.11) | collective-permute-done | bytes 67616 | tf_op jit(solution)/shard_map/ppermute | solution.py:18
  61.9 2.4 %collective-permute-start.13 = (bf16[8,4096]{1,0:T(8,128)(2,1)S(1)}, bf16[8,4096]{1,0:T(8,128)(2,1)S(1)}, u32[]{:S(2)}, u32[]{:S(2)}) collective-permute-start(bf16[8,4096]{1,0:T(8,128)(2,1)S(1)} %shard_map.104), channel_id=1, source_target_pairs={{0,16},{2,18},{4,20},{6,22},{8,24},{10,26},{12,28},{14,30},{16,0},... | collective-permute-start | bytes 196616 | tf_op jit(solution)/shard_map/ppermute | solution.py:18
  67.1 3.3 %collective-permute-done.14 = bf16[8,4096]{1,0:T(8,128)(2,1)S(1)} collective-permute-done((bf16[8,4096]{1,0:T(8,128)(2,1)S(1)}, bf16[8,4096]{1,0:T(8,128)(2,1)S(1)}, u32[]{:S(2)}, u32[]{:S(2)}) %collective-permute-start.14) | collective-permute-done | bytes 65568 | tf_op jit(solution)/shard_map/ppermute | solution.py:18
  73.9 2.9 %collective-permute-done.15.refs_1_ = bf16[32,4096]{1,0:T(8,128)(2,1)S(1)} collective-permute-done((bf16[32,4096]{1,0:T(8,128)(2,1)S(1)}, bf16[32,4096]{1,0:T(8,128)(2,1)S(1)}, u32[]{:S(2)}, u32[]{:S(2)}) %collective-permute-start.15) | collective-permute-done | bytes 262176 | tf_op jit(solution)/shard_map/ppermute | solution.py:18
  76.8 4.3 %collective-permute-done.16.refs_2_ = bf16[32,4096]{1,0:T(8,128)(2,1)S(1)} collective-permute-done((bf16[32,4096]{1,0:T(8,128)(2,1)S(1)}, bf16[32,4096]{1,0:T(8,128)(2,1)S(1)}, u32[]{:S(2)}, u32[]{:S(2)}) %collective-permute-start.16) | collective-permute-done | bytes 262176 | tf_op jit(solution)/shard_map/ppermute | solution.py:18
  81.1 3.3 %out_projection.1.a_ref = bf16[128,512]{1,0:T(8,128)(2,1)S(1)} custom-call(s32[4]{0:T(128)S(1)} %pad_add_fusion.s_ref, bf16[32,4096]{1,0:T(8,128)(2,1)S(1)} %pad_maximum_fusion.1.refs_0_, bf16[32,4096]{1,0:T(8,128)(2,1)S(1)} %collective-permute-done.15.refs_1_, bf16[32,4096]{1,0:T(8,128)(2,1)S(1)} %collective-permute-done.16.refs_2_, ...), custom_call_target="tpu_custom_call" | custom-call | flops 536870912 | bytes 4194304 | tf_op jit(solution)/shard_map/out_projection/pallas_call | solution.py:294
  86.1 2.6 %collective-permute-start.20 = (bf16[72,512]{1,0:T(8,128)(2,1)S(1)}, bf16[72,512]{1,0:T(8,128)(2,1)S(1)}, u32[]{:S(2)}, u32[]{:S(2)}) collective-permute-start(bf16[72,512]{1,0:T(8,128)(2,1)S(1)} %get-tuple-element.23), channel_id=1, source_target_pairs={{0,16},{2,18},{4,20},{6,22},{8,24},{10,26},{12,28},{14,30},{16,0},... | collective-permute-start | bytes 221192 | tf_op jit(solution)/shard_map/ppermute | solution.py:18
  91.7 3.5 %collective-permute-done.20 = bf16[72,512]{1,0:T(8,128)(2,1)S(1)} collective-permute-done((bf16[72,512]{1,0:T(8,128)(2,1)S(1)}, bf16[72,512]{1,0:T(8,128)(2,1)S(1)}, u32[]{:S(2)}, u32[]{:S(2)}) %collective-permute-start.20) | collective-permute-done | bytes 73760 | tf_op jit(solution)/shard_map/ppermute | solution.py:18
  98.7 6.4 %collective-permute-done.26.a_ref = bf16[4,72,512]{2,1,0:T(8,128)(2,1)S(1)} collective-permute-done((bf16[4,72,512]{2,1,0:T(8,128)(2,1)S(1)}, bf16[4,72,512]{2,1,0:T(8,128)(2,1)S(1)}, u32[]{:S(2)}, u32[]{:S(2)}) %collective-permute-start.26) | collective-permute-done | bytes 294944 | tf_op jit(solution)/shard_map/ppermute | solution.py:18
  105.1 3.0 %collective-permute-done.24.a_ref = bf16[4,72,512]{2,1,0:T(8,128)(2,1)S(1)} collective-permute-done((bf16[4,72,512]{2,1,0:T(8,128)(2,1)S(1)}, bf16[4,72,512]{2,1,0:T(8,128)(2,1)S(1)}, u32[]{:S(2)}, u32[]{:S(2)}) %collective-permute-start.24) | collective-permute-done | bytes 294944 | tf_op jit(solution)/shard_map/ppermute | solution.py:18
  109.8 3.1 %shard_map.105 = (f32[128,512]{1,0:T(8,128)S(1)}, f32[128,512]{1,0:T(8,128)S(1)}, f32[8,128]{1,0:T(8,128)S(1)}) custom-call(s32[2]{0:T(128)S(1)} %pad_add_fusion.1.s_ref, bf16[4,72,512]{2,1,0:T(8,128)(2,1)S(1)} %pad_maximum_fusion.a_ref, bf16[4,72,512]{2,1,0:T(8,128)(2,1)S(1)} %collective-permute-done.28.b_ref, bf16[8192,512]{1,0:T(8,128)(2,1)} %gw_hbm.7, ...), custom_call_target="tpu_custom_call" | custom-call | flops 536870912 | bytes 4194304 | tf_op jit(solution)/shard_map/pallas_call | solution.py:421
  112.9 3.1 %shard_map.106 = (f32[128,512]{1,0:T(8,128)S(1)}, f32[128,512]{1,0:T(8,128)S(1)}, f32[8,128]{1,0:T(8,128)S(1)}) custom-call(s32[2]{0:T(128)S(1)} %pad_add_fusion.1.s_ref, bf16[4,72,512]{2,1,0:T(8,128)(2,1)S(1)} %collective-permute-done.26.a_ref, bf16[4,72,512]{2,1,0:T(8,128)(2,1)S(1)} %collective-permute-done.27.b_ref, bf16[8192,512]{1,0:T(8,128)(2,1)} %gw_hbm.7, ...), custom_call_target="tpu_custom_call" | custom-call | flops 536870912 | bytes 4194304 | tf_op jit(solution)/shard_map/pallas_call | solution.py:421
  116.0 3.1 %shard_map.107 = (f32[128,512]{1,0:T(8,128)S(1)}, f32[128,512]{1,0:T(8,128)S(1)}, f32[8,128]{1,0:T(8,128)S(1)}) custom-call(s32[2]{0:T(128)S(1)} %pad_add_fusion.1.s_ref, bf16[4,72,512]{2,1,0:T(8,128)(2,1)S(1)} %collective-permute-done.24.a_ref, bf16[4,72,512]{2,1,0:T(8,128)(2,1)S(1)} %collective-permute-done.25.b_ref, bf16[8192,512]{1,0:T(8,128)(2,1)} %gw_hbm.7, ...), custom_call_target="tpu_custom_call" | custom-call | flops 536870912 | bytes 4194304 | tf_op jit(solution)/shard_map/pallas_call | solution.py:421
  119.1 3.1 %shard_map.108 = (bf16[64,512]{1,0:T(8,128)(2,1)S(1)}, bf16[64,512]{1,0:T(8,128)(2,1)S(1)}) custom-call(s32[2]{0:T(128)S(1)} %pad_add_fusion.1.s_ref, bf16[4,72,512]{2,1,0:T(8,128)(2,1)S(1)} %collective-permute-done.22.a_ref, bf16[4,72,512]{2,1,0:T(8,128)(2,1)S(1)} %collective-permute-done.23.b_ref, bf16[8192,512]{1,0:T(8,128)(2,1)} %gw_hbm.7, ...), custom_call_target="tpu_custom_call" | custom-call | flops 536870912 | bytes 4194304 | tf_op jit(solution)/shard_map/pallas_call | solution.py:421
  122.2 3.0 %collective-permute-start.34 = (bf16[64,512]{1,0:T(8,128)(2,1)S(1)}, bf16[64,512]{1,0:T(8,128)(2,1)S(1)}, u32[]{:S(2)}, u32[]{:S(2)}) collective-permute-start(bf16[64,512]{1,0:T(8,128)(2,1)S(1)} %get-tuple-element.34), channel_id=1, source_target_pairs={{0,8},{2,10},{4,12},{6,14},{8,0},{10,2},{12,4},{14,6},{16,24},{18,... | collective-permute-start | bytes 196616 | tf_op jit(solution)/shard_map/ppermute | solution.py:18
  125.3 2.3 %collective-permute-start.36 = (bf16[64,512]{1,0:T(8,128)(2,1)S(1)}, bf16[64,512]{1,0:T(8,128)(2,1)S(1)}, u32[]{:S(2)}, u32[]{:S(2)}) collective-permute-start(bf16[64,512]{1,0:T(8,128)(2,1)S(1)} %get-tuple-element.34), channel_id=1, source_target_pairs={{0,24},{2,26},{4,28},{6,30},{8,16},{10,18},{12,20},{14,22},{16,8},... | collective-permute-start | bytes 196616 | tf_op jit(solution)/shard_map/ppermute | solution.py:18
  129.7 2.3 %collective-permute-start.31 = (bf16[64,512]{1,0:T(8,128)(2,1)S(1)}, bf16[64,512]{1,0:T(8,128)(2,1)S(1)}, u32[]{:S(2)}, u32[]{:S(2)}) collective-permute-start(bf16[64,512]{1,0:T(8,128)(2,1)S(1)} %get-tuple-element.33), channel_id=1, source_target_pairs={{0,24},{2,26},{4,28},{6,30},{8,16},{10,18},{12,20},{14,22},{16,8},... | collective-permute-start | bytes 196616 | tf_op jit(solution)/shard_map/ppermute | solution.py:18
  135.2 3.8 %collective-permute-done.30 = bf16[64,512]{1,0:T(8,128)(2,1)S(1)} collective-permute-done((bf16[64,512]{1,0:T(8,128)(2,1)S(1)}, bf16[64,512]{1,0:T(8,128)(2,1)S(1)}, u32[]{:S(2)}, u32[]{:S(2)}) %collective-permute-start.30) | collective-permute-done | bytes 65568 | tf_op jit(solution)/shard_map/ppermute | solution.py:18
  143.7 4.7 %collective-permute-done.32.refs_0_ = bf16[4,64,512]{2,1,0:T(8,128)(2,1)S(1)} collective-permute-done((bf16[4,64,512]{2,1,0:T(8,128)(2,1)S(1)}, bf16[4,64,512]{2,1,0:T(8,128)(2,1)S(1)}, u32[]{:S(2)}, u32[]{:S(2)}) %collective-permute-start.32) | collective-permute-done | bytes 262176 | tf_op jit(solution)/shard_map/ppermute | solution.py:18
  149.3 2.3 %shard_map.109.refs_3_ = f32[128,512]{1,0:T(8,128)S(1)} custom-call(s32[2]{0:T(128)S(1)} %pad_add_fusion.1.s_ref, bf16[4,64,512]{2,1,0:T(8,128)(2,1)S(1)} %pad_maximum_fusion.2.refs_0_, bf16[4,64,512]{2,1,0:T(8,128)(2,1)S(1)} %pad_maximum_fusion.3.refs_1_, bf16[8192,512]{1,0:T(8,128)(2,1)} %refs_2_.7), custom_call_target="tpu_custom_call" | custom-call | flops 268435456 | bytes 2097152 | tf_op jit(solution)/shard_map/pallas_call | solution.py:468
  151.7 2.3 %shard_map.110.refs_3_ = f32[128,512]{1,0:T(8,128)S(1)} custom-call(s32[2]{0:T(128)S(1)} %pad_add_fusion.1.s_ref, bf16[4,64,512]{2,1,0:T(8,128)(2,1)S(1)} %collective-permute-done.40.refs_0_, bf16[4,64,512]{2,1,0:T(8,128)(2,1)S(1)} %collective-permute-done.37.refs_1_, bf16[8192,512]{1,0:T(8,128)(2,1)} %refs_2_.7, f32[128,512]{1,0:T(8,128)S(1)} %shard_map.109.refs_3_), custom_call_target="tpu_custom_call" | custom-call | flops 268435456 | bytes 2097152 | tf_op jit(solution)/shard_map/pallas_call | solution.py:468
  154.0 2.3 %shard_map.111.refs_3_ = f32[128,512]{1,0:T(8,128)S(1)} custom-call(s32[2]{0:T(128)S(1)} %pad_add_fusion.1.s_ref, bf16[4,64,512]{2,1,0:T(8,128)(2,1)S(1)} %collective-permute-done.32.refs_0_, bf16[4,64,512]{2,1,0:T(8,128)(2,1)S(1)} %collective-permute-done.39.refs_1_, bf16[8192,512]{1,0:T(8,128)(2,1)} %refs_2_.7, f32[128,512]{1,0:T(8,128)S(1)} %shard_map.110.refs_3_), custom_call_target="tpu_custom_call" | custom-call | flops 268435456 | bytes 2097152 | tf_op jit(solution)/shard_map/pallas_call | solution.py:468
  158.0 2.3 %shard_map.112 = bf16[128,512]{1,0:T(8,128)(2,1)S(1)} custom-call(s32[2]{0:T(128)S(1)} %pad_add_fusion.1.s_ref, bf16[4,64,512]{2,1,0:T(8,128)(2,1)S(1)} %collective-permute-done.33.refs_0_, bf16[4,64,512]{2,1,0:T(8,128)(2,1)S(1)} %collective-permute-done.38.refs_1_, bf16[8192,512]{1,0:T(8,128)(2,1)} %refs_2_.7, f32[128,512]{1,0:T(8,128)S(1)} %shard_map.111.refs_3_), custom_call_target="tpu_custom_call" | custom-call | flops 268435456 | bytes 2097152 | tf_op jit(solution)/shard_map/pallas_call | solution.py:468
  (87 shorter events, 43.3 us)
Async XLA Ops:
  0.0 6.6 %collective-permute-start = (bf16[8,4096]{1,0:T(8,128)(2,1)}, bf16[8,4096]{1,0:T(8,128)(2,1)S(1)}, u32[]{:S(2)}, u32[]{:S(2)}) collective-permute-start(bf16[8,4096]{1,0:T(8,128)(2,1)} %param.10), channel_id=1, source_target_pairs={{0,8},{2,10},{4,12},{6,14},{8,0},{10,2},{12,4},{14,6},{16,24},{18,... | collective-permute-start | bytes 196616 | tf_op jit(solution)/shard_map/ppermute | solution.py:18
  3.1 7.5 %collective-permute-start.1 = (bf16[8,4096]{1,0:T(8,128)(2,1)}, bf16[8,4096]{1,0:T(8,128)(2,1)S(1)}, u32[]{:S(2)}, u32[]{:S(2)}) collective-permute-start(bf16[8,4096]{1,0:T(8,128)(2,1)} %param.10), channel_id=1, source_target_pairs={{0,16},{2,18},{4,20},{6,22},{8,24},{10,26},{12,28},{14,30},{16,0},... | collective-permute-start | bytes 196616 | tf_op jit(solution)/shard_map/ppermute | solution.py:18
  12.0 10.2 %collective-permute-start.3 = (bf16[32,4096]{1,0:T(8,128)(2,1)S(1)}, bf16[32,4096]{1,0:T(8,128)(2,1)S(1)}, u32[]{:S(2)}, u32[]{:S(2)}) collective-permute-start(bf16[32,4096]{1,0:T(8,128)(2,1)S(1)} %constant_dynamic-update-slice_fusion.refs_0_), channel_id=1, source_target_pairs={{0,2},{2,0},{4,6},{6,4},{8,10},{10,8},{12,14},{14,12},{16,18},{18,... | collective-permute-start | bytes 786440 | tf_op jit(solution)/shard_map/ppermute | solution.py:18
  13.5 8.7 %collective-permute-start.4 = (bf16[32,4096]{1,0:T(8,128)(2,1)S(1)}, bf16[32,4096]{1,0:T(8,128)(2,1)S(1)}, u32[]{:S(2)}, u32[]{:S(2)}) collective-permute-start(bf16[32,4096]{1,0:T(8,128)(2,1)S(1)} %constant_dynamic-update-slice_fusion.refs_0_), channel_id=1, source_target_pairs={{0,4},{2,6},{4,0},{6,2},{8,12},{10,14},{12,8},{14,10},{16,20},{18,... | collective-permute-start | bytes 786440 | tf_op jit(solution)/shard_map/ppermute | solution.py:18
  21.7 14.6 %collective-permute-start.7 = (bf16[32,4096]{1,0:T(8,128)(2,1)S(1)}, bf16[32,4096]{1,0:T(8,128)(2,1)S(1)}, u32[]{:S(2)}, u32[]{:S(2)}) collective-permute-start(bf16[32,4096]{1,0:T(8,128)(2,1)S(1)} %constant_dynamic-update-slice_fusion.refs_0_), channel_id=1, source_target_pairs={{0,6},{2,4},{4,2},{6,0},{8,14},{10,12},{12,10},{14,8},{16,22},{18,... | collective-permute-start | bytes 786440 | tf_op jit(solution)/shard_map/ppermute | solution.py:18
  33.0 19.0 %collective-permute-start.5 = (bf16[32,4224]{1,0:T(8,128)(2,1)S(1)}, bf16[32,4224]{1,0:T(8,128)(2,1)S(1)}, u32[]{:S(2)}, u32[]{:S(2)}) collective-permute-start(bf16[32,4224]{1,0:T(8,128)(2,1)S(1)} %get-tuple-element.20), channel_id=1, source_target_pairs={{0,2},{2,0},{4,6},{6,4},{8,10},{10,8},{12,14},{14,12},{16,18},{18,... | collective-permute-start | bytes 811016 | tf_op jit(solution)/shard_map/ppermute | solution.py:18
  34.6 17.5 %collective-permute-start.6 = (bf16[32,4224]{1,0:T(8,128)(2,1)S(1)}, bf16[32,4224]{1,0:T(8,128)(2,1)S(1)}, u32[]{:S(2)}, u32[]{:S(2)}) collective-permute-start(bf16[32,4224]{1,0:T(8,128)(2,1)S(1)} %get-tuple-element.21), channel_id=1, source_target_pairs={{0,4},{2,6},{4,0},{6,2},{8,12},{10,14},{12,8},{14,10},{16,20},{18,... | collective-permute-start | bytes 811016 | tf_op jit(solution)/shard_map/ppermute | solution.py:18
  44.0 8.1 %collective-permute-start.8 = (bf16[32,4224]{1,0:T(8,128)(2,1)S(1)}, bf16[32,4224]{1,0:T(8,128)(2,1)S(1)}, u32[]{:S(2)}, u32[]{:S(2)}) collective-permute-start(bf16[32,4224]{1,0:T(8,128)(2,1)S(1)} %shard_map.102), channel_id=1, source_target_pairs={{0,6},{2,4},{4,2},{6,0},{8,14},{10,12},{12,10},{14,8},{16,22},{18,... | collective-permute-start | bytes 811016 | tf_op jit(solution)/shard_map/ppermute | solution.py:18
  55.0 6.5 %collective-permute-start.11 = (bf16[8,4224]{1,0:T(8,128)(2,1)S(1)}, bf16[8,4224]{1,0:T(8,128)(2,1)S(1)}, u32[]{:S(2)}, u32[]{:S(2)}) collective-permute-start(bf16[8,4224]{1,0:T(8,128)(2,1)S(1)} %get-tuple-element.35), channel_id=1, source_target_pairs={{0,24},{2,26},{4,28},{6,30},{8,16},{10,18},{12,20},{14,22},{16,8},... | collective-permute-start | bytes 202760 | tf_op jit(solution)/shard_map/ppermute | solution.py:18
  70.4 6.4 %collective-permute-start.15 = (bf16[32,4096]{1,0:T(8,128)(2,1)S(1)}, bf16[32,4096]{1,0:T(8,128)(2,1)S(1)}, u32[]{:S(2)}, u32[]{:S(2)}) collective-permute-start(bf16[32,4096]{1,0:T(8,128)(2,1)S(1)} %pad_maximum_fusion.1.refs_0_), channel_id=1, source_target_pairs={{0,2},{2,0},{4,6},{6,4},{8,10},{10,8},{12,14},{14,12},{16,18},{18,... | collective-permute-start | bytes 786440 | tf_op jit(solution)/shard_map/ppermute | solution.py:18
  71.9 9.2 %collective-permute-start.16 = (bf16[32,4096]{1,0:T(8,128)(2,1)S(1)}, bf16[32,4096]{1,0:T(8,128)(2,1)S(1)}, u32[]{:S(2)}, u32[]{:S(2)}) collective-permute-start(bf16[32,4096]{1,0:T(8,128)(2,1)S(1)} %pad_maximum_fusion.1.refs_0_), channel_id=1, source_target_pairs={{0,4},{2,6},{4,0},{6,2},{8,12},{10,14},{12,8},{14,10},{16,20},{18,... | collective-permute-start | bytes 786440 | tf_op jit(solution)/shard_map/ppermute | solution.py:18
  73.5 7.7 %collective-permute-start.17 = (bf16[32,4096]{1,0:T(8,128)(2,1)S(1)}, bf16[32,4096]{1,0:T(8,128)(2,1)S(1)}, u32[]{:S(2)}, u32[]{:S(2)}) collective-permute-start(bf16[32,4096]{1,0:T(8,128)(2,1)S(1)} %pad_maximum_fusion.1.refs_0_), channel_id=1, source_target_pairs={{0,6},{2,4},{4,2},{6,0},{8,14},{10,12},{12,10},{14,8},{16,22},{18,... | collective-permute-start | bytes 786440 | tf_op jit(solution)/shard_map/ppermute | solution.py:18
  86.1 9.0 %collective-permute-start.20 = (bf16[72,512]{1,0:T(8,128)(2,1)S(1)}, bf16[72,512]{1,0:T(8,128)(2,1)S(1)}, u32[]{:S(2)}, u32[]{:S(2)}) collective-permute-start(bf16[72,512]{1,0:T(8,128)(2,1)S(1)} %get-tuple-element.23), channel_id=1, source_target_pairs={{0,16},{2,18},{4,20},{6,22},{8,24},{10,26},{12,28},{14,30},{16,0},... | collective-permute-start | bytes 221192 | tf_op jit(solution)/shard_map/ppermute | solution.py:18
  95.2 9.9 %collective-permute-start.26 = (bf16[4,72,512]{2,1,0:T(8,128)(2,1)S(1)}, bf16[4,72,512]{2,1,0:T(8,128)(2,1)S(1)}, u32[]{:S(2)}, u32[]{:S(2)}) collective-permute-start(bf16[4,72,512]{2,1,0:T(8,128)(2,1)S(1)} %pad_maximum_fusion.a_ref), channel_id=1, source_target_pairs={{0,2},{2,0},{4,6},{6,4},{8,10},{10,8},{12,14},{14,12},{16,18},{18,... | collective-permute-start | bytes 884744 | tf_op jit(solution)/shard_map/ppermute | solution.py:18
  96.2 11.9 %collective-permute-start.24 = (bf16[4,72,512]{2,1,0:T(8,128)(2,1)S(1)}, bf16[4,72,512]{2,1,0:T(8,128)(2,1)S(1)}, u32[]{:S(2)}, u32[]{:S(2)}) collective-permute-start(bf16[4,72,512]{2,1,0:T(8,128)(2,1)S(1)} %pad_maximum_fusion.a_ref), channel_id=1, source_target_pairs={{0,4},{2,6},{4,0},{6,2},{8,12},{10,14},{12,8},{14,10},{16,20},{18,... | collective-permute-start | bytes 884744 | tf_op jit(solution)/shard_map/ppermute | solution.py:18
  97.3 12.4 %collective-permute-start.22 = (bf16[4,72,512]{2,1,0:T(8,128)(2,1)S(1)}, bf16[4,72,512]{2,1,0:T(8,128)(2,1)S(1)}, u32[]{:S(2)}, u32[]{:S(2)}) collective-permute-start(bf16[4,72,512]{2,1,0:T(8,128)(2,1)S(1)} %pad_maximum_fusion.a_ref), channel_id=1, source_target_pairs={{0,6},{2,4},{4,2},{6,0},{8,14},{10,12},{12,10},{14,8},{16,22},{18,... | collective-permute-start | bytes 884744 | tf_op jit(solution)/shard_map/ppermute | solution.py:18
  98.7 11.1 %collective-permute-start.28 = (bf16[4,72,512]{2,1,0:T(8,128)(2,1)S(1)}, bf16[4,72,512]{2,1,0:T(8,128)(2,1)S(1)}, u32[]{:S(2)}, u32[]{:S(2)}) collective-permute-start(bf16[4,72,512]{2,1,0:T(8,128)(2,1)S(1)} %pad_maximum_fusion.a_ref), channel_id=1, source_target_pairs={{0,1},{1,0},{2,3},{3,2},{4,5},{5,4},{6,7},{7,6},{8,9},{9,8},{10,11... | collective-permute-start | bytes 884744 | tf_op jit(solution)/shard_map/ppermute | solution.py:23
  105.1 7.8 %collective-permute-start.27 = (bf16[4,72,512]{2,1,0:T(8,128)(2,1)S(1)}, bf16[4,72,512]{2,1,0:T(8,128)(2,1)S(1)}, u32[]{:S(2)}, u32[]{:S(2)}) collective-permute-start(bf16[4,72,512]{2,1,0:T(8,128)(2,1)S(1)} %collective-permute-done.26.a_ref), channel_id=1, source_target_pairs={{0,1},{1,0},{2,3},{3,2},{4,5},{5,4},{6,7},{7,6},{8,9},{9,8},{10,11... | collective-permute-start | bytes 884744 | tf_op jit(solution)/shard_map/ppermute | solution.py:23
  108.1 7.9 %collective-permute-start.25 = (bf16[4,72,512]{2,1,0:T(8,128)(2,1)S(1)}, bf16[4,72,512]{2,1,0:T(8,128)(2,1)S(1)}, u32[]{:S(2)}, u32[]{:S(2)}) collective-permute-start(bf16[4,72,512]{2,1,0:T(8,128)(2,1)S(1)} %collective-permute-done.24.a_ref), channel_id=1, source_target_pairs={{0,1},{1,0},{2,3},{3,2},{4,5},{5,4},{6,7},{7,6},{8,9},{9,8},{10,11... | collective-permute-start | bytes 884744 | tf_op jit(solution)/shard_map/ppermute | solution.py:23
  109.7 9.3 %collective-permute-start.23 = (bf16[4,72,512]{2,1,0:T(8,128)(2,1)S(1)}, bf16[4,72,512]{2,1,0:T(8,128)(2,1)S(1)}, u32[]{:S(2)}, u32[]{:S(2)}) collective-permute-start(bf16[4,72,512]{2,1,0:T(8,128)(2,1)S(1)} %collective-permute-done.22.a_ref), channel_id=1, source_target_pairs={{0,1},{1,0},{2,3},{3,2},{4,5},{5,4},{6,7},{7,6},{8,9},{9,8},{10,11... | collective-permute-start | bytes 884744 | tf_op jit(solution)/shard_map/ppermute | solution.py:23
  122.2 7.5 %collective-permute-start.34 = (bf16[64,512]{1,0:T(8,128)(2,1)S(1)}, bf16[64,512]{1,0:T(8,128)(2,1)S(1)}, u32[]{:S(2)}, u32[]{:S(2)}) collective-permute-start(bf16[64,512]{1,0:T(8,128)(2,1)S(1)} %get-tuple-element.34), channel_id=1, source_target_pairs={{0,8},{2,10},{4,12},{6,14},{8,0},{10,2},{12,4},{14,6},{16,24},{18,... | collective-permute-start | bytes 196616 | tf_op jit(solution)/shard_map/ppermute | solution.py:18
  125.2 8.7 %collective-permute-start.35 = (bf16[64,512]{1,0:T(8,128)(2,1)S(1)}, bf16[64,512]{1,0:T(8,128)(2,1)S(1)}, u32[]{:S(2)}, u32[]{:S(2)}) collective-permute-start(bf16[64,512]{1,0:T(8,128)(2,1)S(1)} %get-tuple-element.34), channel_id=1, source_target_pairs={{0,16},{2,18},{4,20},{6,22},{8,24},{10,26},{12,28},{14,30},{16,0},... | collective-permute-start | bytes 196616 | tf_op jit(solution)/shard_map/ppermute | solution.py:18
  125.3 8.6 %collective-permute-start.36 = (bf16[64,512]{1,0:T(8,128)(2,1)S(1)}, bf16[64,512]{1,0:T(8,128)(2,1)S(1)}, u32[]{:S(2)}, u32[]{:S(2)}) collective-permute-start(bf16[64,512]{1,0:T(8,128)(2,1)S(1)} %get-tuple-element.34), channel_id=1, source_target_pairs={{0,24},{2,26},{4,28},{6,30},{8,16},{10,18},{12,20},{14,22},{16,8},... | collective-permute-start | bytes 196616 | tf_op jit(solution)/shard_map/ppermute | solution.py:18
  127.6 7.6 %collective-permute-start.29 = (bf16[64,512]{1,0:T(8,128)(2,1)S(1)}, bf16[64,512]{1,0:T(8,128)(2,1)S(1)}, u32[]{:S(2)}, u32[]{:S(2)}) collective-permute-start(bf16[64,512]{1,0:T(8,128)(2,1)S(1)} %get-tuple-element.33), channel_id=1, source_target_pairs={{0,8},{2,10},{4,12},{6,14},{8,0},{10,2},{12,4},{14,6},{16,24},{18,... | collective-permute-start | bytes 196616 | tf_op jit(solution)/shard_map/ppermute | solution.py:18
  128.7 10.4 %collective-permute-start.30 = (bf16[64,512]{1,0:T(8,128)(2,1)S(1)}, bf16[64,512]{1,0:T(8,128)(2,1)S(1)}, u32[]{:S(2)}, u32[]{:S(2)}) collective-permute-start(bf16[64,512]{1,0:T(8,128)(2,1)S(1)} %get-tuple-element.33), channel_id=1, source_target_pairs={{0,16},{2,18},{4,20},{6,22},{8,24},{10,26},{12,28},{14,30},{16,0},... | collective-permute-start | bytes 196616 | tf_op jit(solution)/shard_map/ppermute | solution.py:18
  129.7 9.3 %collective-permute-start.31 = (bf16[64,512]{1,0:T(8,128)(2,1)S(1)}, bf16[64,512]{1,0:T(8,128)(2,1)S(1)}, u32[]{:S(2)}, u32[]{:S(2)}) collective-permute-start(bf16[64,512]{1,0:T(8,128)(2,1)S(1)} %get-tuple-element.33), channel_id=1, source_target_pairs={{0,24},{2,26},{4,28},{6,30},{8,16},{10,18},{12,20},{14,22},{16,8},... | collective-permute-start | bytes 196616 | tf_op jit(solution)/shard_map/ppermute | solution.py:18
  133.9 8.2 %collective-permute-start.37 = (bf16[4,64,512]{2,1,0:T(8,128)(2,1)S(1)}, bf16[4,64,512]{2,1,0:T(8,128)(2,1)S(1)}, u32[]{:S(2)}, u32[]{:S(2)}) collective-permute-start(bf16[4,64,512]{2,1,0:T(8,128)(2,1)S(1)} %pad_maximum_fusion.3.refs_1_), channel_id=1, source_target_pairs={{0,2},{2,0},{4,6},{6,4},{8,10},{10,8},{12,14},{14,12},{16,18},{18,... | collective-permute-start | bytes 786440 | tf_op jit(solution)/shard_map/ppermute | solution.py:18
  139.1 9.2 %collective-permute-start.32 = (bf16[4,64,512]{2,1,0:T(8,128)(2,1)S(1)}, bf16[4,64,512]{2,1,0:T(8,128)(2,1)S(1)}, u32[]{:S(2)}, u32[]{:S(2)}) collective-permute-start(bf16[4,64,512]{2,1,0:T(8,128)(2,1)S(1)} %pad_maximum_fusion.2.refs_0_), channel_id=1, source_target_pairs={{0,4},{2,6},{4,0},{6,2},{8,12},{10,14},{12,8},{14,10},{16,20},{18,... | collective-permute-start | bytes 786440 | tf_op jit(solution)/shard_map/ppermute | solution.py:18
  140.1 11.5 %collective-permute-start.40 = (bf16[4,64,512]{2,1,0:T(8,128)(2,1)S(1)}, bf16[4,64,512]{2,1,0:T(8,128)(2,1)S(1)}, u32[]{:S(2)}, u32[]{:S(2)}) collective-permute-start(bf16[4,64,512]{2,1,0:T(8,128)(2,1)S(1)} %pad_maximum_fusion.2.refs_0_), channel_id=1, source_target_pairs={{0,2},{2,0},{4,6},{6,4},{8,10},{10,8},{12,14},{14,12},{16,18},{18,... | collective-permute-start | bytes 786440 | tf_op jit(solution)/shard_map/ppermute | solution.py:18
  141.6 12.4 %collective-permute-start.39 = (bf16[4,64,512]{2,1,0:T(8,128)(2,1)S(1)}, bf16[4,64,512]{2,1,0:T(8,128)(2,1)S(1)}, u32[]{:S(2)}, u32[]{:S(2)}) collective-permute-start(bf16[4,64,512]{2,1,0:T(8,128)(2,1)S(1)} %pad_maximum_fusion.3.refs_1_), channel_id=1, source_target_pairs={{0,4},{2,6},{4,0},{6,2},{8,12},{10,14},{12,8},{14,10},{16,20},{18,... | collective-permute-start | bytes 786440 | tf_op jit(solution)/shard_map/ppermute | solution.py:18
  142.1 15.8 %collective-permute-start.38 = (bf16[4,64,512]{2,1,0:T(8,128)(2,1)S(1)}, bf16[4,64,512]{2,1,0:T(8,128)(2,1)S(1)}, u32[]{:S(2)}, u32[]{:S(2)}) collective-permute-start(bf16[4,64,512]{2,1,0:T(8,128)(2,1)S(1)} %collective-permute-done.37.refs_1_), channel_id=1, source_target_pairs={{0,4},{2,6},{4,0},{6,2},{8,12},{10,14},{12,8},{14,10},{16,20},{18,... | collective-permute-start | bytes 786440 | tf_op jit(solution)/shard_map/ppermute | solution.py:18
  148.3 9.6 %collective-permute-start.33 = (bf16[4,64,512]{2,1,0:T(8,128)(2,1)S(1)}, bf16[4,64,512]{2,1,0:T(8,128)(2,1)S(1)}, u32[]{:S(2)}, u32[]{:S(2)}) collective-permute-start(bf16[4,64,512]{2,1,0:T(8,128)(2,1)S(1)} %collective-permute-done.32.refs_0_), channel_id=1, source_target_pairs={{0,2},{2,0},{4,6},{6,4},{8,10},{10,8},{12,14},{14,12},{16,18},{18,... | collective-permute-start | bytes 786440 | tf_op jit(solution)/shard_map/ppermute | solution.py:18
  (13 other events, 124.6 us)
where the time goes:
time: 163 us; the launch traced here: 162 us
  Pallas kernels  52.5 us (32%)
  waiting for transfers between devices  52 us (32%)
  starting transfers between devices  49.1 us (30%)
  local copies, waits for them, and re-layouts  7.56 us (5%)
    ppermute x36, waiting for transfers between devices, xor_blk(): return lax.ppermute(x, 'blk', [(i, i ^ mask) for i in range(blocks)])  49.3 us
    ppermute x36, starting transfers between devices, xor_blk(): return lax.ppermute(x, 'blk', [(i, i ^ mask) for i in range(blocks)])  49 us
    pallas_call x3, Pallas kernels, attention(): pl.pallas_call(kernel, grid_spec=pltpu.PrefetchScalarGridSpec(num_scalar_...  26.2 us
    pallas_call x4, Pallas kernels, feed_chunk(): pl.pallas_call(kernel, grid_spec=pltpu.PrefetchScalarGridSpec(num_scalar_...  12.3 us
    pallas_call x4, Pallas kernels, down_chunk(): pl.pallas_call(kernel, grid_spec=pltpu.PrefetchScalarGridSpec(num_scalar_...  9.33 us
    transpose x1, local copies, waits for them, and re-layouts, body(): values = stay(jnp.transpose(value_cache, (0, 2, 1, 3)))  6.59 us
    pallas_call x1, Pallas kernels, out_projection(): pl.pallas_call(kernel, grid_spec=pltpu.PrefetchScalarGridSpec(num_scalar_...  3.32 us
  transfers between devices with their start and end apart: 42, of which 19 were waited for; matrix products, arithmetic and copies ran while one was open for 5% of the time, Pallas kernels for 26%

commit v1 on v0

--- a/solution.py
+++ b/solution.py
@@ -271,12 +271,7 @@
     steps = depth // step
 
     def kernel(s_ref, *refs):
-        ins, w_hbm, o_ref, w_all, sems = refs[:count], refs[count], refs[count + 1], refs[count + 2], refs[count + 3]
-        copies = [
-            pltpu.make_async_copy(w_hbm.at[pl.ds(k * step, step)], w_all.at[k], sems.at[k]) for k in range(steps)
-        ]
-        for c in copies:
-            c.start()
+        ins, w_ref, o_ref = refs[:count], refs[count], refs[count + 1]
         there = lax.broadcasted_iota(jnp.int32, (rows, rows), 0)
         here = lax.broadcasted_iota(jnp.int32, (rows, rows), 1)
         piece = here // rows_dev
@@ -287,8 +282,7 @@
         for k in range(steps):
             rel = jnp.concatenate([r[:, k * step : (k + 1) * step] for r in ins], axis=0)
             lhs = jnp.dot(order, rel, preferred_element_type=f32).astype(bf16)
-            copies[k].wait()
-            acc += jnp.dot(lhs, w_all[k], preferred_element_type=f32)
+            acc += jnp.dot(lhs, w_ref[k * step : (k + 1) * step, :], preferred_element_type=f32)
         o_ref[...] = acc.astype(bf16)
 
     return pl.pallas_call(
@@ -297,9 +291,8 @@
             num_scalar_prefetch=1,
             grid=(1,),
             in_specs=[pl.BlockSpec((chunk_rows, depth), lambda k, s: (0, 0))] * count
-            + [pl.BlockSpec(memory_space=pltpu.HBM)],
+            + [pl.BlockSpec(weight.shape, lambda k, s: (0, 0), pipeline_mode=pl.Buffered(1))],
             out_specs=pl.BlockSpec((rows, columns), lambda k, s: (0, 0)),
-            scratch_shapes=[pltpu.VMEM((steps, step, columns), bf16), pltpu.SemaphoreType.DMA((steps,))],
         ),
         out_shape=jax.ShapeDtypeStruct((rows, columns), bf16),
         compiler_params=pltpu.CompilerParams(vmem_limit_bytes=24 << 20),
@@ -449,20 +442,13 @@
     columns = weight.shape[1]
 
     def kernel(s_ref, *refs):
-        h_refs, w_hbm, rest = refs[: len(halves)], refs[len(halves)], refs[len(halves) + 1 :]
-        w_all, sems = rest[-2:]
-        copies = []
-        for k in range(far):
-            at = pl.ds(pl.multiple_of((s_ref[0] ^ (k * near + part)) * units, units), units)
-            copies.append(pltpu.make_async_copy(w_hbm.at[at], w_all.at[k], sems.at[k]))
-        for c in copies:
-            c.start()
+        h_refs, w_ref, rest = refs[: len(halves)], refs[len(halves)], refs[len(halves) + 1 :]
         acc = jnp.zeros((rows, columns), f32) if carry is None else rest[0][...]
         for k in range(far):
             lhs = jnp.concatenate([h[k] for h in h_refs], axis=0)
-            copies[k].wait()
-            acc += jnp.dot(lhs, w_all[k], preferred_element_type=f32)
-        rest[-3][...] = acc.astype(rest[-3].dtype)
+            at = pl.ds(pl.multiple_of((s_ref[0] ^ (k * near + part)) * units, units), units)
+            acc += jnp.dot(lhs, w_ref[at, :], preferred_element_type=f32)
+        rest[-1][...] = acc.astype(rest[-1].dtype)
 
     flat = lambda shape: pl.BlockSpec(shape, lambda i, s: (0,) * len(shape))
     return pl.pallas_call(
@@ -471,10 +457,9 @@
             num_scalar_prefetch=1,
             grid=(1,),
             in_specs=[flat(h.shape) for h in halves]
-            + [pl.BlockSpec(memory_space=pltpu.HBM)]
+            + [pl.BlockSpec(weight.shape, lambda i, s: (0, 0), pipeline_mode=pl.Buffered(1))]
             + ([flat((rows, columns))] if carry is not None else []),
             out_specs=flat((rows, columns)),
-            scratch_shapes=[pltpu.VMEM((far, units, columns), bf16), pltpu.SemaphoreType.DMA((far,))],
         ),
         out_shape=jax.ShapeDtypeStruct((rows, columns), bf16 if last else f32),
         compiler_params=pltpu.CompilerParams(vmem_limit_bytes=20 << 20),
@@ -513,9 +498,7 @@
     stack_join = lambda parts: jnp.stack(parts, axis=0)
 
     stay = lambda x: pltpu.with_memory_space_constraint(x, pltpu.HBM)
-    out_weight, gate_weight, up_weight, down_weight = map(
-        stay, (out_weight, gate_weight, up_weight, down_weight)
-    )
+    gate_weight, up_weight = stay(gate_weight), stay(up_weight)
     keys = stay(jnp.transpose(key_cache, (0, 2, 1, 3)))
     values = stay(jnp.transpose(value_cache, (0, 2, 1, 3)))
     asked = gather(queries, near, far, blocks, rows_join)

time: 163 us -> 160 us (0.982)
  Pallas kernels: 52.5 us -> 46.2 us
  waiting for transfers between devices: 52 us -> 55.7 us
    pallas_call x4, Pallas kernels: 9.33 us -> 3.93 us  [down_chunk(): pl.pallas_call(kernel, grid_spec=pltpu.PrefetchScalarGridSpec(num_scalar_...]
    ppermute x36, waiting for transfers between devices: 49.3 us -> 53.1 us  [xor_blk(): return lax.ppermute(x, 'blk', [(i, i ^ mask) for i in range(blocks)])]
  transfers between devices with their start and end apart: 42 -> 42, of which waited for: 19 -> 20; matrix products, arithmetic and copies ran while one was open for 5% -> 5% of each run, Pallas kernels for 26% -> 24%
where the time goes in v1:
time: 160 us
  waiting for transfers between devices  55.7 us (35%)
  starting transfers between devices  49.1 us (31%)
  Pallas kernels  46.2 us (29%)
  local copies, waits for them, and re-layouts  7.61 us (5%)
    ppermute x36, waiting for transfers between devices, xor_blk(): return lax.ppermute(x, 'blk', [(i, i ^ mask) for i in range(blocks)])  53.1 us
    ppermute x36, starting transfers between devices, xor_blk(): return lax.ppermute(x, 'blk', [(i, i ^ mask) for i in range(blocks)])  48.9 us
    pallas_call x3, Pallas kernels, attention(): pl.pallas_call(kernel, grid_spec=pltpu.PrefetchScalarGridSpec(num_scalar_...  26.6 us
    pallas_call x4, Pallas kernels, feed_chunk(): pl.pallas_call(kernel, grid_spec=pltpu.PrefetchScalarGridSpec(num_scalar_...  12.6 us
    transpose x1, local copies, waits for them, and re-layouts, body(): values = stay(jnp.transpose(value_cache, (0, 2, 1, 3)))  6.62 us
    pallas_call x4, Pallas kernels, down_chunk(): pl.pallas_call(kernel, grid_spec=pltpu.PrefetchScalarGridSpec(num_scalar_...  3.93 us
  transfers between devices with their start and end apart: 42, of which 20 were waited for; matrix products, arithmetic and copies ran while one was open for 5% of the time, Pallas kernels for 24%

profile of v1, /device:TPU:0, one launch (start us, length us, event | category | flops | bytes accessed | tf_op | source)
XLA Modules:
  0.0 159.9 jit_solution(11363590358149405799)
XLA Ops:
  0.0 3.1 %collective-permute-start = (bf16[8,4096]{1,0:T(8,128)(2,1)}, bf16[8,4096]{1,0:T(8,128)(2,1)S(1)}, u32[]{:S(2)}, u32[]{:S(2)}) collective-permute-start(bf16[8,4096]{1,0:T(8,128)(2,1)} %param.10), channel_id=1, source_target_pairs={{0,8},{2,10},{4,12},{6,14},{8,0},{10,2},{12,4},{14,6},{16,24},{18,... | collective-permute-start | bytes 196616 | tf_op jit(solution)/shard_map/ppermute | solution.py:18
  3.1 2.6 %collective-permute-start.1 = (bf16[8,4096]{1,0:T(8,128)(2,1)}, bf16[8,4096]{1,0:T(8,128)(2,1)S(1)}, u32[]{:S(2)}, u32[]{:S(2)}) collective-permute-start(bf16[8,4096]{1,0:T(8,128)(2,1)} %param.10), channel_id=1, source_target_pairs={{0,16},{2,18},{4,20},{6,22},{8,24},{10,26},{12,28},{14,30},{16,0},... | collective-permute-start | bytes 196616 | tf_op jit(solution)/shard_map/ppermute | solution.py:18
  6.6 4.0 %collective-permute-done.1 = bf16[8,4096]{1,0:T(8,128)(2,1)S(1)} collective-permute-done((bf16[8,4096]{1,0:T(8,128)(2,1)}, bf16[8,4096]{1,0:T(8,128)(2,1)S(1)}, u32[]{:S(2)}, u32[]{:S(2)}) %collective-permute-start.1) | collective-permute-done | bytes 65568 | tf_op jit(solution)/shard_map/ppermute | solution.py:18
  15.0 6.6 %copy_bitcast_fusion = (bf16[2,4,2048,128]{3,2,1,0:T(8,128)(2,1)}, bf16[2,4,2048,128]{3,2,1,0:T(8,128)(2,1)}) fusion(bf16[2,2048,4,128]{3,2,1,0:T(4,128)(2,1)} %param.12, bf16[2,2048,4,128]{3,2,1,0:T(4,128)(2,1)} %param.11), kind=kLoop, calls=%fused_computation | loop fusion | bytes 16777216 | tf_op jit(solution)/shard_map/transpose | solution.py:503
  22.2 10.8 %shard_map.101 = (bf16[32,4224]{1,0:T(8,128)(2,1)S(1)}, bf16[32,4224]{1,0:T(8,128)(2,1)S(1)}) custom-call(s32[4]{0:T(128)S(1)} %pad_add_fusion.s_ref, bf16[32,4096]{1,0:T(8,128)(2,1)S(1)} %collective-permute-done.3.refs_0_, bf16[32,4096]{1,0:T(8,128)(2,1)S(1)} %collective-permute-done.4.refs_1_, bf16[2,4,2048,128]{3,2,1,0:T(8,128)(2,1)} %get-tuple-element.40.refs_1_.refs_2_, ...), custom_call_target="tpu_custom_call" | custom-call | flops 4294967296 | bytes 8388608 | tf_op jit(solution)/shard_map/pallas_call | solution.py:200
  34.6 1.8 %collective-permute-start.6 = (bf16[32,4224]{1,0:T(8,128)(2,1)S(1)}, bf16[32,4224]{1,0:T(8,128)(2,1)S(1)}, u32[]{:S(2)}, u32[]{:S(2)}) collective-permute-start(bf16[32,4224]{1,0:T(8,128)(2,1)S(1)} %get-tuple-element.21), channel_id=1, source_target_pairs={{0,4},{2,6},{4,0},{6,2},{8,12},{10,14},{12,8},{14,10},{16,20},{18,... | collective-permute-start | bytes 811016 | tf_op jit(solution)/shard_map/ppermute | solution.py:18
  36.4 7.6 %shard_map.102 = bf16[32,4224]{1,0:T(8,128)(2,1)S(1)} custom-call(s32[4]{0:T(128)S(1)} %pad_add_fusion.s_ref, bf16[32,4096]{1,0:T(8,128)(2,1)S(1)} %collective-permute-done.7.refs_0_, bf16[2,4,2048,128]{3,2,1,0:T(8,128)(2,1)} %get-tuple-element.40.refs_1_.refs_2_, bf16[2,4,2048,128]{3,2,1,0:T(8,128)(2,1)} %get-tuple-element.39.refs_2_.refs_3_), custom_call_target="tpu_custom_call" | custom-call | flops 2147483648 | bytes 8388608 | tf_op jit(solution)/shard_map/pallas_call | solution.py:200
  44.3 8.2 %shard_map.100.refs_0_ = bf16[32,4224]{1,0:T(8,128)(2,1)S(1)} custom-call(s32[4]{0:T(128)S(1)} %pad_add_fusion.s_ref, bf16[32,4096]{1,0:T(8,128)(2,1)S(1)} %constant_dynamic-update-slice_fusion.refs_0_, bf16[2,4,2048,128]{3,2,1,0:T(8,128)(2,1)} %get-tuple-element.40.refs_1_.refs_2_, bf16[2,4,2048,128]{3,2,1,0:T(8,128)(2,1)} %get-tuple-element.39.refs_2_.refs_3_), custom_call_target="tpu_custom_call" | custom-call | flops 2147483648 | bytes 8388608 | tf_op jit(solution)/shard_map/pallas_call | solution.py:200
  53.3 1.8 %collective-permute-start.10 = (bf16[8,4224]{1,0:T(8,128)(2,1)S(1)}, bf16[8,4224]{1,0:T(8,128)(2,1)S(1)}, u32[]{:S(2)}, u32[]{:S(2)}) collective-permute-start(bf16[8,4224]{1,0:T(8,128)(2,1)S(1)} %get-tuple-element.36), channel_id=1, source_target_pairs={{0,16},{2,18},{4,20},{6,22},{8,24},{10,26},{12,28},{14,30},{16,0},... | collective-permute-start | bytes 202760 | tf_op jit(solution)/shard_map/ppermute | solution.py:18
  56.9 2.2 %collective-permute-done.10.refs_2_ = bf16[8,4224]{1,0:T(8,128)(2,1)S(1)} collective-permute-done((bf16[8,4224]{1,0:T(8,128)(2,1)S(1)}, bf16[8,4224]{1,0:T(8,128)(2,1)S(1)}, u32[]{:S(2)}, u32[]{:S(2)}) %collective-permute-start.10) | collective-permute-done | bytes 67616 | tf_op jit(solution)/shard_map/ppermute | solution.py:18
  59.1 2.3 %collective-permute-done.11.refs_3_ = bf16[8,4224]{1,0:T(8,128)(2,1)S(1)} collective-permute-done((bf16[8,4224]{1,0:T(8,128)(2,1)S(1)}, bf16[8,4224]{1,0:T(8,128)(2,1)S(1)}, u32[]{:S(2)}, u32[]{:S(2)}) %collective-permute-start.11) | collective-permute-done | bytes 67616 | tf_op jit(solution)/shard_map/ppermute | solution.py:18
  62.2 2.3 %collective-permute-start.13 = (bf16[8,4096]{1,0:T(8,128)(2,1)S(1)}, bf16[8,4096]{1,0:T(8,128)(2,1)S(1)}, u32[]{:S(2)}, u32[]{:S(2)}) collective-permute-start(bf16[8,4096]{1,0:T(8,128)(2,1)S(1)} %shard_map.104), channel_id=1, source_target_pairs={{0,16},{2,18},{4,20},{6,22},{8,24},{10,26},{12,28},{14,30},{16,0},... | collective-permute-start | bytes 196616 | tf_op jit(solution)/shard_map/ppermute | solution.py:18
  67.4 3.2 %collective-permute-done.14 = bf16[8,4096]{1,0:T(8,128)(2,1)S(1)} collective-permute-done((bf16[8,4096]{1,0:T(8,128)(2,1)S(1)}, bf16[8,4096]{1,0:T(8,128)(2,1)S(1)}, u32[]{:S(2)}, u32[]{:S(2)}) %collective-permute-start.14) | collective-permute-done | bytes 65568 | tf_op jit(solution)/shard_map/ppermute | solution.py:18
  74.1 2.9 %collective-permute-done.15.refs_1_ = bf16[32,4096]{1,0:T(8,128)(2,1)S(1)} collective-permute-done((bf16[32,4096]{1,0:T(8,128)(2,1)S(1)}, bf16[32,4096]{1,0:T(8,128)(2,1)S(1)}, u32[]{:S(2)}, u32[]{:S(2)}) %collective-permute-start.15) | collective-permute-done | bytes 262176 | tf_op jit(solution)/shard_map/ppermute | solution.py:18
  77.0 4.1 %collective-permute-done.16.refs_2_ = bf16[32,4096]{1,0:T(8,128)(2,1)S(1)} collective-permute-done((bf16[32,4096]{1,0:T(8,128)(2,1)S(1)}, bf16[32,4096]{1,0:T(8,128)(2,1)S(1)}, u32[]{:S(2)}, u32[]{:S(2)}) %collective-permute-start.16) | collective-permute-done | bytes 262176 | tf_op jit(solution)/shard_map/ppermute | solution.py:18
  84.6 2.6 %collective-permute-start.20 = (bf16[72,512]{1,0:T(8,128)(2,1)S(1)}, bf16[72,512]{1,0:T(8,128)(2,1)S(1)}, u32[]{:S(2)}, u32[]{:S(2)}) collective-permute-start(bf16[72,512]{1,0:T(8,128)(2,1)S(1)} %get-tuple-element.23), channel_id=1, source_target_pairs={{0,16},{2,18},{4,20},{6,22},{8,24},{10,26},{12,28},{14,30},{16,0},... | collective-permute-start | bytes 221192 | tf_op jit(solution)/shard_map/ppermute | solution.py:18
  87.2 1.8 %collective-permute-start.21 = (bf16[72,512]{1,0:T(8,128)(2,1)S(1)}, bf16[72,512]{1,0:T(8,128)(2,1)S(1)}, u32[]{:S(2)}, u32[]{:S(2)}) collective-permute-start(bf16[72,512]{1,0:T(8,128)(2,1)S(1)} %get-tuple-element.23), channel_id=1, source_target_pairs={{0,24},{2,26},{4,28},{6,30},{8,16},{10,18},{12,20},{14,22},{16,8},... | collective-permute-start | bytes 221192 | tf_op jit(solution)/shard_map/ppermute | solution.py:18
  90.1 3.5 %collective-permute-done.20 = bf16[72,512]{1,0:T(8,128)(2,1)S(1)} collective-permute-done((bf16[72,512]{1,0:T(8,128)(2,1)S(1)}, bf16[72,512]{1,0:T(8,128)(2,1)S(1)}, u32[]{:S(2)}, u32[]{:S(2)}) %collective-permute-start.20) | collective-permute-done | bytes 73760 | tf_op jit(solution)/shard_map/ppermute | solution.py:18
  97.2 6.4 %collective-permute-done.26.a_ref = bf16[4,72,512]{2,1,0:T(8,128)(2,1)S(1)} collective-permute-done((bf16[4,72,512]{2,1,0:T(8,128)(2,1)S(1)}, bf16[4,72,512]{2,1,0:T(8,128)(2,1)S(1)}, u32[]{:S(2)}, u32[]{:S(2)}) %collective-permute-start.26) | collective-permute-done | bytes 294944 | tf_op jit(solution)/shard_map/ppermute | solution.py:18
  103.6 3.0 %collective-permute-done.24.a_ref = bf16[4,72,512]{2,1,0:T(8,128)(2,1)S(1)} collective-permute-done((bf16[4,72,512]{2,1,0:T(8,128)(2,1)S(1)}, bf16[4,72,512]{2,1,0:T(8,128)(2,1)S(1)}, u32[]{:S(2)}, u32[]{:S(2)}) %collective-permute-start.24) | collective-permute-done | bytes 294944 | tf_op jit(solution)/shard_map/ppermute | solution.py:18
  108.3 3.1 %shard_map.105 = (f32[128,512]{1,0:T(8,128)S(1)}, f32[128,512]{1,0:T(8,128)S(1)}, f32[8,128]{1,0:T(8,128)S(1)}) custom-call(s32[2]{0:T(128)S(1)} %pad_add_fusion.1.s_ref, bf16[4,72,512]{2,1,0:T(8,128)(2,1)S(1)} %pad_maximum_fusion.a_ref, bf16[4,72,512]{2,1,0:T(8,128)(2,1)S(1)} %collective-permute-done.28.b_ref, bf16[8192,512]{1,0:T(8,128)(2,1)} %gw_hbm.7, ...), custom_call_target="tpu_custom_call" | custom-call | flops 536870912 | bytes 4194304 | tf_op jit(solution)/shard_map/pallas_call | solution.py:414
  111.4 3.1 %shard_map.106 = (f32[128,512]{1,0:T(8,128)S(1)}, f32[128,512]{1,0:T(8,128)S(1)}, f32[8,128]{1,0:T(8,128)S(1)}) custom-call(s32[2]{0:T(128)S(1)} %pad_add_fusion.1.s_ref, bf16[4,72,512]{2,1,0:T(8,128)(2,1)S(1)} %collective-permute-done.26.a_ref, bf16[4,72,512]{2,1,0:T(8,128)(2,1)S(1)} %collective-permute-done.27.b_ref, bf16[8192,512]{1,0:T(8,128)(2,1)} %gw_hbm.7, ...), custom_call_target="tpu_custom_call" | custom-call | flops 536870912 | bytes 4194304 | tf_op jit(solution)/shard_map/pallas_call | solution.py:414
  114.5 3.1 %shard_map.107 = (f32[128,512]{1,0:T(8,128)S(1)}, f32[128,512]{1,0:T(8,128)S(1)}, f32[8,128]{1,0:T(8,128)S(1)}) custom-call(s32[2]{0:T(128)S(1)} %pad_add_fusion.1.s_ref, bf16[4,72,512]{2,1,0:T(8,128)(2,1)S(1)} %collective-permute-done.24.a_ref, bf16[4,72,512]{2,1,0:T(8,128)(2,1)S(1)} %collective-permute-done.25.b_ref, bf16[8192,512]{1,0:T(8,128)(2,1)} %gw_hbm.7, ...), custom_call_target="tpu_custom_call" | custom-call | flops 536870912 | bytes 4194304 | tf_op jit(solution)/shard_map/pallas_call | solution.py:414
  117.6 3.4 %shard_map.108 = (bf16[64,512]{1,0:T(8,128)(2,1)S(1)}, bf16[64,512]{1,0:T(8,128)(2,1)S(1)}) custom-call(s32[2]{0:T(128)S(1)} %pad_add_fusion.1.s_ref, bf16[4,72,512]{2,1,0:T(8,128)(2,1)S(1)} %collective-permute-done.22.a_ref, bf16[4,72,512]{2,1,0:T(8,128)(2,1)S(1)} %collective-permute-done.23.b_ref, bf16[8192,512]{1,0:T(8,128)(2,1)} %gw_hbm.7, ...), custom_call_target="tpu_custom_call" | custom-call | flops 536870912 | bytes 4194304 | tf_op jit(solution)/shard_map/pallas_call | solution.py:414
  120.9 3.0 %collective-permute-start.34 = (bf16[64,512]{1,0:T(8,128)(2,1)S(1)}, bf16[64,512]{1,0:T(8,128)(2,1)S(1)}, u32[]{:S(2)}, u32[]{:S(2)}) collective-permute-start(bf16[64,512]{1,0:T(8,128)(2,1)S(1)} %get-tuple-element.34), channel_id=1, source_target_pairs={{0,8},{2,10},{4,12},{6,14},{8,0},{10,2},{12,4},{14,6},{16,24},{18,... | collective-permute-start | bytes 196616 | tf_op jit(solution)/shard_map/ppermute | solution.py:18
  124.1 2.3 %collective-permute-start.36 = (bf16[64,512]{1,0:T(8,128)(2,1)S(1)}, bf16[64,512]{1,0:T(8,128)(2,1)S(1)}, u32[]{:S(2)}, u32[]{:S(2)}) collective-permute-start(bf16[64,512]{1,0:T(8,128)(2,1)S(1)} %get-tuple-element.34), channel_id=1, source_target_pairs={{0,24},{2,26},{4,28},{6,30},{8,16},{10,18},{12,20},{14,22},{16,8},... | collective-permute-start | bytes 196616 | tf_op jit(solution)/shard_map/ppermute | solution.py:18
  128.5 2.3 %collective-permute-start.31 = (bf16[64,512]{1,0:T(8,128)(2,1)S(1)}, bf16[64,512]{1,0:T(8,128)(2,1)S(1)}, u32[]{:S(2)}, u32[]{:S(2)}) collective-permute-start(bf16[64,512]{1,0:T(8,128)(2,1)S(1)} %get-tuple-element.33), channel_id=1, source_target_pairs={{0,24},{2,26},{4,28},{6,30},{8,16},{10,18},{12,20},{14,22},{16,8},... | collective-permute-start | bytes 196616 | tf_op jit(solution)/shard_map/ppermute | solution.py:18
  130.8 1.9 %collective-permute-done.35 = bf16[64,512]{1,0:T(8,128)(2,1)S(1)} collective-permute-done((bf16[64,512]{1,0:T(8,128)(2,1)S(1)}, bf16[64,512]{1,0:T(8,128)(2,1)S(1)}, u32[]{:S(2)}, u32[]{:S(2)}) %collective-permute-start.35) | collective-permute-done | bytes 65568 | tf_op jit(solution)/shard_map/ppermute | solution.py:18
  134.0 3.9 %collective-permute-done.30 = bf16[64,512]{1,0:T(8,128)(2,1)S(1)} collective-permute-done((bf16[64,512]{1,0:T(8,128)(2,1)S(1)}, bf16[64,512]{1,0:T(8,128)(2,1)S(1)}, u32[]{:S(2)}, u32[]{:S(2)}) %collective-permute-start.30) | collective-permute-done | bytes 65568 | tf_op jit(solution)/shard_map/ppermute | solution.py:18
  142.4 4.7 %collective-permute-done.32.refs_0_ = bf16[4,64,512]{2,1,0:T(8,128)(2,1)S(1)} collective-permute-done((bf16[4,64,512]{2,1,0:T(8,128)(2,1)S(1)}, bf16[4,64,512]{2,1,0:T(8,128)(2,1)S(1)}, u32[]{:S(2)}, u32[]{:S(2)}) %collective-permute-start.32) | collective-permute-done | bytes 262176 | tf_op jit(solution)/shard_map/ppermute | solution.py:18
  150.0 2.7 %collective-permute-done.39.refs_1_ = bf16[4,64,512]{2,1,0:T(8,128)(2,1)S(1)} collective-permute-done((bf16[4,64,512]{2,1,0:T(8,128)(2,1)S(1)}, bf16[4,64,512]{2,1,0:T(8,128)(2,1)S(1)}, u32[]{:S(2)}, u32[]{:S(2)}) %collective-permute-start.39) | collective-permute-done | bytes 262176 | tf_op jit(solution)/shard_map/ppermute | solution.py:18
  153.7 3.0 %collective-permute-done.38.refs_1_ = bf16[4,64,512]{2,1,0:T(8,128)(2,1)S(1)} collective-permute-done((bf16[4,64,512]{2,1,0:T(8,128)(2,1)S(1)}, bf16[4,64,512]{2,1,0:T(8,128)(2,1)S(1)}, u32[]{:S(2)}, u32[]{:S(2)}) %collective-permute-start.38) | collective-permute-done | bytes 262176 | tf_op jit(solution)/shard_map/ppermute | solution.py:18
  (94 shorter events, 42.7 us)
Async XLA Ops:
  0.0 6.6 %collective-permute-start = (bf16[8,4096]{1,0:T(8,128)(2,1)}, bf16[8,4096]{1,0:T(8,128)(2,1)S(1)}, u32[]{:S(2)}, u32[]{:S(2)}) collective-permute-start(bf16[8,4096]{1,0:T(8,128)(2,1)} %param.10), channel_id=1, source_target_pairs={{0,8},{2,10},{4,12},{6,14},{8,0},{10,2},{12,4},{14,6},{16,24},{18,... | collective-permute-start | bytes 196616 | tf_op jit(solution)/shard_map/ppermute | solution.py:18
  3.1 7.5 %collective-permute-start.1 = (bf16[8,4096]{1,0:T(8,128)(2,1)}, bf16[8,4096]{1,0:T(8,128)(2,1)S(1)}, u32[]{:S(2)}, u32[]{:S(2)}) collective-permute-start(bf16[8,4096]{1,0:T(8,128)(2,1)} %param.10), channel_id=1, source_target_pairs={{0,16},{2,18},{4,20},{6,22},{8,24},{10,26},{12,28},{14,30},{16,0},... | collective-permute-start | bytes 196616 | tf_op jit(solution)/shard_map/ppermute | solution.py:18
  12.0 10.3 %collective-permute-start.3 = (bf16[32,4096]{1,0:T(8,128)(2,1)S(1)}, bf16[32,4096]{1,0:T(8,128)(2,1)S(1)}, u32[]{:S(2)}, u32[]{:S(2)}) collective-permute-start(bf16[32,4096]{1,0:T(8,128)(2,1)S(1)} %constant_dynamic-update-slice_fusion.refs_0_), channel_id=1, source_target_pairs={{0,2},{2,0},{4,6},{6,4},{8,10},{10,8},{12,14},{14,12},{16,18},{18,... | collective-permute-start | bytes 786440 | tf_op jit(solution)/shard_map/ppermute | solution.py:18
  13.5 8.7 %collective-permute-start.4 = (bf16[32,4096]{1,0:T(8,128)(2,1)S(1)}, bf16[32,4096]{1,0:T(8,128)(2,1)S(1)}, u32[]{:S(2)}, u32[]{:S(2)}) collective-permute-start(bf16[32,4096]{1,0:T(8,128)(2,1)S(1)} %constant_dynamic-update-slice_fusion.refs_0_), channel_id=1, source_target_pairs={{0,4},{2,6},{4,0},{6,2},{8,12},{10,14},{12,8},{14,10},{16,20},{18,... | collective-permute-start | bytes 786440 | tf_op jit(solution)/shard_map/ppermute | solution.py:18
  21.7 14.6 %collective-permute-start.7 = (bf16[32,4096]{1,0:T(8,128)(2,1)S(1)}, bf16[32,4096]{1,0:T(8,128)(2,1)S(1)}, u32[]{:S(2)}, u32[]{:S(2)}) collective-permute-start(bf16[32,4096]{1,0:T(8,128)(2,1)S(1)} %constant_dynamic-update-slice_fusion.refs_0_), channel_id=1, source_target_pairs={{0,6},{2,4},{4,2},{6,0},{8,14},{10,12},{12,10},{14,8},{16,22},{18,... | collective-permute-start | bytes 786440 | tf_op jit(solution)/shard_map/ppermute | solution.py:18
  33.0 19.4 %collective-permute-start.5 = (bf16[32,4224]{1,0:T(8,128)(2,1)S(1)}, bf16[32,4224]{1,0:T(8,128)(2,1)S(1)}, u32[]{:S(2)}, u32[]{:S(2)}) collective-permute-start(bf16[32,4224]{1,0:T(8,128)(2,1)S(1)} %get-tuple-element.20), channel_id=1, source_target_pairs={{0,2},{2,0},{4,6},{6,4},{8,10},{10,8},{12,14},{14,12},{16,18},{18,... | collective-permute-start | bytes 811016 | tf_op jit(solution)/shard_map/ppermute | solution.py:18
  34.6 17.9 %collective-permute-start.6 = (bf16[32,4224]{1,0:T(8,128)(2,1)S(1)}, bf16[32,4224]{1,0:T(8,128)(2,1)S(1)}, u32[]{:S(2)}, u32[]{:S(2)}) collective-permute-start(bf16[32,4224]{1,0:T(8,128)(2,1)S(1)} %get-tuple-element.21), channel_id=1, source_target_pairs={{0,4},{2,6},{4,0},{6,2},{8,12},{10,14},{12,8},{14,10},{16,20},{18,... | collective-permute-start | bytes 811016 | tf_op jit(solution)/shard_map/ppermute | solution.py:18
  44.0 8.5 %collective-permute-start.8 = (bf16[32,4224]{1,0:T(8,128)(2,1)S(1)}, bf16[32,4224]{1,0:T(8,128)(2,1)S(1)}, u32[]{:S(2)}, u32[]{:S(2)}) collective-permute-start(bf16[32,4224]{1,0:T(8,128)(2,1)S(1)} %shard_map.102), channel_id=1, source_target_pairs={{0,6},{2,4},{4,2},{6,0},{8,14},{10,12},{12,10},{14,8},{16,22},{18,... | collective-permute-start | bytes 811016 | tf_op jit(solution)/shard_map/ppermute | solution.py:18
  70.6 6.4 %collective-permute-start.15 = (bf16[32,4096]{1,0:T(8,128)(2,1)S(1)}, bf16[32,4096]{1,0:T(8,128)(2,1)S(1)}, u32[]{:S(2)}, u32[]{:S(2)}) collective-permute-start(bf16[32,4096]{1,0:T(8,128)(2,1)S(1)} %pad_maximum_fusion.1.refs_0_), channel_id=1, source_target_pairs={{0,2},{2,0},{4,6},{6,4},{8,10},{10,8},{12,14},{14,12},{16,18},{18,... | collective-permute-start | bytes 786440 | tf_op jit(solution)/shard_map/ppermute | solution.py:18
  72.0 9.2 %collective-permute-start.16 = (bf16[32,4096]{1,0:T(8,128)(2,1)S(1)}, bf16[32,4096]{1,0:T(8,128)(2,1)S(1)}, u32[]{:S(2)}, u32[]{:S(2)}) collective-permute-start(bf16[32,4096]{1,0:T(8,128)(2,1)S(1)} %pad_maximum_fusion.1.refs_0_), channel_id=1, source_target_pairs={{0,4},{2,6},{4,0},{6,2},{8,12},{10,14},{12,8},{14,10},{16,20},{18,... | collective-permute-start | bytes 786440 | tf_op jit(solution)/shard_map/ppermute | solution.py:18
  73.5 7.7 %collective-permute-start.17 = (bf16[32,4096]{1,0:T(8,128)(2,1)S(1)}, bf16[32,4096]{1,0:T(8,128)(2,1)S(1)}, u32[]{:S(2)}, u32[]{:S(2)}) collective-permute-start(bf16[32,4096]{1,0:T(8,128)(2,1)S(1)} %pad_maximum_fusion.1.refs_0_), channel_id=1, source_target_pairs={{0,6},{2,4},{4,2},{6,0},{8,14},{10,12},{12,10},{14,8},{16,22},{18,... | collective-permute-start | bytes 786440 | tf_op jit(solution)/shard_map/ppermute | solution.py:18
  84.6 9.0 %collective-permute-start.20 = (bf16[72,512]{1,0:T(8,128)(2,1)S(1)}, bf16[72,512]{1,0:T(8,128)(2,1)S(1)}, u32[]{:S(2)}, u32[]{:S(2)}) collective-permute-start(bf16[72,512]{1,0:T(8,128)(2,1)S(1)} %get-tuple-element.23), channel_id=1, source_target_pairs={{0,16},{2,18},{4,20},{6,22},{8,24},{10,26},{12,28},{14,30},{16,0},... | collective-permute-start | bytes 221192 | tf_op jit(solution)/shard_map/ppermute | solution.py:18
  87.2 6.4 %collective-permute-start.21 = (bf16[72,512]{1,0:T(8,128)(2,1)S(1)}, bf16[72,512]{1,0:T(8,128)(2,1)S(1)}, u32[]{:S(2)}, u32[]{:S(2)}) collective-permute-start(bf16[72,512]{1,0:T(8,128)(2,1)S(1)} %get-tuple-element.23), channel_id=1, source_target_pairs={{0,24},{2,26},{4,28},{6,30},{8,16},{10,18},{12,20},{14,22},{16,8},... | collective-permute-start | bytes 221192 | tf_op jit(solution)/shard_map/ppermute | solution.py:18
  93.6 9.9 %collective-permute-start.26 = (bf16[4,72,512]{2,1,0:T(8,128)(2,1)S(1)}, bf16[4,72,512]{2,1,0:T(8,128)(2,1)S(1)}, u32[]{:S(2)}, u32[]{:S(2)}) collective-permute-start(bf16[4,72,512]{2,1,0:T(8,128)(2,1)S(1)} %pad_maximum_fusion.a_ref), channel_id=1, source_target_pairs={{0,2},{2,0},{4,6},{6,4},{8,10},{10,8},{12,14},{14,12},{16,18},{18,... | collective-permute-start | bytes 884744 | tf_op jit(solution)/shard_map/ppermute | solution.py:18
  94.7 11.9 %collective-permute-start.24 = (bf16[4,72,512]{2,1,0:T(8,128)(2,1)S(1)}, bf16[4,72,512]{2,1,0:T(8,128)(2,1)S(1)}, u32[]{:S(2)}, u32[]{:S(2)}) collective-permute-start(bf16[4,72,512]{2,1,0:T(8,128)(2,1)S(1)} %pad_maximum_fusion.a_ref), channel_id=1, source_target_pairs={{0,4},{2,6},{4,0},{6,2},{8,12},{10,14},{12,8},{14,10},{16,20},{18,... | collective-permute-start | bytes 884744 | tf_op jit(solution)/shard_map/ppermute | solution.py:18
  95.8 12.4 %collective-permute-start.22 = (bf16[4,72,512]{2,1,0:T(8,128)(2,1)S(1)}, bf16[4,72,512]{2,1,0:T(8,128)(2,1)S(1)}, u32[]{:S(2)}, u32[]{:S(2)}) collective-permute-start(bf16[4,72,512]{2,1,0:T(8,128)(2,1)S(1)} %pad_maximum_fusion.a_ref), channel_id=1, source_target_pairs={{0,6},{2,4},{4,2},{6,0},{8,14},{10,12},{12,10},{14,8},{16,22},{18,... | collective-permute-start | bytes 884744 | tf_op jit(solution)/shard_map/ppermute | solution.py:18
  97.2 11.1 %collective-permute-start.28 = (bf16[4,72,512]{2,1,0:T(8,128)(2,1)S(1)}, bf16[4,72,512]{2,1,0:T(8,128)(2,1)S(1)}, u32[]{:S(2)}, u32[]{:S(2)}) collective-permute-start(bf16[4,72,512]{2,1,0:T(8,128)(2,1)S(1)} %pad_maximum_fusion.a_ref), channel_id=1, source_target_pairs={{0,1},{1,0},{2,3},{3,2},{4,5},{5,4},{6,7},{7,6},{8,9},{9,8},{10,11... | collective-permute-start | bytes 884744 | tf_op jit(solution)/shard_map/ppermute | solution.py:23
  103.6 7.8 %collective-permute-start.27 = (bf16[4,72,512]{2,1,0:T(8,128)(2,1)S(1)}, bf16[4,72,512]{2,1,0:T(8,128)(2,1)S(1)}, u32[]{:S(2)}, u32[]{:S(2)}) collective-permute-start(bf16[4,72,512]{2,1,0:T(8,128)(2,1)S(1)} %collective-permute-done.26.a_ref), channel_id=1, source_target_pairs={{0,1},{1,0},{2,3},{3,2},{4,5},{5,4},{6,7},{7,6},{8,9},{9,8},{10,11... | collective-permute-start | bytes 884744 | tf_op jit(solution)/shard_map/ppermute | solution.py:23
  106.6 7.9 %collective-permute-start.25 = (bf16[4,72,512]{2,1,0:T(8,128)(2,1)S(1)}, bf16[4,72,512]{2,1,0:T(8,128)(2,1)S(1)}, u32[]{:S(2)}, u32[]{:S(2)}) collective-permute-start(bf16[4,72,512]{2,1,0:T(8,128)(2,1)S(1)} %collective-permute-done.24.a_ref), channel_id=1, source_target_pairs={{0,1},{1,0},{2,3},{3,2},{4,5},{5,4},{6,7},{7,6},{8,9},{9,8},{10,11... | collective-permute-start | bytes 884744 | tf_op jit(solution)/shard_map/ppermute | solution.py:23
  108.2 9.4 %collective-permute-start.23 = (bf16[4,72,512]{2,1,0:T(8,128)(2,1)S(1)}, bf16[4,72,512]{2,1,0:T(8,128)(2,1)S(1)}, u32[]{:S(2)}, u32[]{:S(2)}) collective-permute-start(bf16[4,72,512]{2,1,0:T(8,128)(2,1)S(1)} %collective-permute-done.22.a_ref), channel_id=1, source_target_pairs={{0,1},{1,0},{2,3},{3,2},{4,5},{5,4},{6,7},{7,6},{8,9},{9,8},{10,11... | collective-permute-start | bytes 884744 | tf_op jit(solution)/shard_map/ppermute | solution.py:23
  120.9 7.5 %collective-permute-start.34 = (bf16[64,512]{1,0:T(8,128)(2,1)S(1)}, bf16[64,512]{1,0:T(8,128)(2,1)S(1)}, u32[]{:S(2)}, u32[]{:S(2)}) collective-permute-start(bf16[64,512]{1,0:T(8,128)(2,1)S(1)} %get-tuple-element.34), channel_id=1, source_target_pairs={{0,8},{2,10},{4,12},{6,14},{8,0},{10,2},{12,4},{14,6},{16,24},{18,... | collective-permute-start | bytes 196616 | tf_op jit(solution)/shard_map/ppermute | solution.py:18
  123.9 8.7 %collective-permute-start.35 = (bf16[64,512]{1,0:T(8,128)(2,1)S(1)}, bf16[64,512]{1,0:T(8,128)(2,1)S(1)}, u32[]{:S(2)}, u32[]{:S(2)}) collective-permute-start(bf16[64,512]{1,0:T(8,128)(2,1)S(1)} %get-tuple-element.34), channel_id=1, source_target_pairs={{0,16},{2,18},{4,20},{6,22},{8,24},{10,26},{12,28},{14,30},{16,0},... | collective-permute-start | bytes 196616 | tf_op jit(solution)/shard_map/ppermute | solution.py:18
  124.1 8.6 %collective-permute-start.36 = (bf16[64,512]{1,0:T(8,128)(2,1)S(1)}, bf16[64,512]{1,0:T(8,128)(2,1)S(1)}, u32[]{:S(2)}, u32[]{:S(2)}) collective-permute-start(bf16[64,512]{1,0:T(8,128)(2,1)S(1)} %get-tuple-element.34), channel_id=1, source_target_pairs={{0,24},{2,26},{4,28},{6,30},{8,16},{10,18},{12,20},{14,22},{16,8},... | collective-permute-start | bytes 196616 | tf_op jit(solution)/shard_map/ppermute | solution.py:18
  126.4 7.6 %collective-permute-start.29 = (bf16[64,512]{1,0:T(8,128)(2,1)S(1)}, bf16[64,512]{1,0:T(8,128)(2,1)S(1)}, u32[]{:S(2)}, u32[]{:S(2)}) collective-permute-start(bf16[64,512]{1,0:T(8,128)(2,1)S(1)} %get-tuple-element.33), channel_id=1, source_target_pairs={{0,8},{2,10},{4,12},{6,14},{8,0},{10,2},{12,4},{14,6},{16,24},{18,... | collective-permute-start | bytes 196616 | tf_op jit(solution)/shard_map/ppermute | solution.py:18
  127.4 10.4 %collective-permute-start.30 = (bf16[64,512]{1,0:T(8,128)(2,1)S(1)}, bf16[64,512]{1,0:T(8,128)(2,1)S(1)}, u32[]{:S(2)}, u32[]{:S(2)}) collective-permute-start(bf16[64,512]{1,0:T(8,128)(2,1)S(1)} %get-tuple-element.33), channel_id=1, source_target_pairs={{0,16},{2,18},{4,20},{6,22},{8,24},{10,26},{12,28},{14,30},{16,0},... | collective-permute-start | bytes 196616 | tf_op jit(solution)/shard_map/ppermute | solution.py:18
  128.5 9.3 %collective-permute-start.31 = (bf16[64,512]{1,0:T(8,128)(2,1)S(1)}, bf16[64,512]{1,0:T(8,128)(2,1)S(1)}, u32[]{:S(2)}, u32[]{:S(2)}) collective-permute-start(bf16[64,512]{1,0:T(8,128)(2,1)S(1)} %get-tuple-element.33), channel_id=1, source_target_pairs={{0,24},{2,26},{4,28},{6,30},{8,16},{10,18},{12,20},{14,22},{16,8},... | collective-permute-start | bytes 196616 | tf_op jit(solution)/shard_map/ppermute | solution.py:18
  132.7 8.2 %collective-permute-start.37 = (bf16[4,64,512]{2,1,0:T(8,128)(2,1)S(1)}, bf16[4,64,512]{2,1,0:T(8,128)(2,1)S(1)}, u32[]{:S(2)}, u32[]{:S(2)}) collective-permute-start(bf16[4,64,512]{2,1,0:T(8,128)(2,1)S(1)} %pad_maximum_fusion.3.refs_1_), channel_id=1, source_target_pairs={{0,2},{2,0},{4,6},{6,4},{8,10},{10,8},{12,14},{14,12},{16,18},{18,... | collective-permute-start | bytes 786440 | tf_op jit(solution)/shard_map/ppermute | solution.py:18
  137.9 9.2 %collective-permute-start.32 = (bf16[4,64,512]{2,1,0:T(8,128)(2,1)S(1)}, bf16[4,64,512]{2,1,0:T(8,128)(2,1)S(1)}, u32[]{:S(2)}, u32[]{:S(2)}) collective-permute-start(bf16[4,64,512]{2,1,0:T(8,128)(2,1)S(1)} %pad_maximum_fusion.2.refs_0_), channel_id=1, source_target_pairs={{0,4},{2,6},{4,0},{6,2},{8,12},{10,14},{12,8},{14,10},{16,20},{18,... | collective-permute-start | bytes 786440 | tf_op jit(solution)/shard_map/ppermute | solution.py:18
  138.9 10.1 %collective-permute-start.40 = (bf16[4,64,512]{2,1,0:T(8,128)(2,1)S(1)}, bf16[4,64,512]{2,1,0:T(8,128)(2,1)S(1)}, u32[]{:S(2)}, u32[]{:S(2)}) collective-permute-start(bf16[4,64,512]{2,1,0:T(8,128)(2,1)S(1)} %pad_maximum_fusion.2.refs_0_), channel_id=1, source_target_pairs={{0,2},{2,0},{4,6},{6,4},{8,10},{10,8},{12,14},{14,12},{16,18},{18,... | collective-permute-start | bytes 786440 | tf_op jit(solution)/shard_map/ppermute | solution.py:18
  140.4 12.3 %collective-permute-start.39 = (bf16[4,64,512]{2,1,0:T(8,128)(2,1)S(1)}, bf16[4,64,512]{2,1,0:T(8,128)(2,1)S(1)}, u32[]{:S(2)}, u32[]{:S(2)}) collective-permute-start(bf16[4,64,512]{2,1,0:T(8,128)(2,1)S(1)} %pad_maximum_fusion.3.refs_1_), channel_id=1, source_target_pairs={{0,4},{2,6},{4,0},{6,2},{8,12},{10,14},{12,8},{14,10},{16,20},{18,... | collective-permute-start | bytes 786440 | tf_op jit(solution)/shard_map/ppermute | solution.py:18
  140.9 15.9 %collective-permute-start.38 = (bf16[4,64,512]{2,1,0:T(8,128)(2,1)S(1)}, bf16[4,64,512]{2,1,0:T(8,128)(2,1)S(1)}, u32[]{:S(2)}, u32[]{:S(2)}) collective-permute-start(bf16[4,64,512]{2,1,0:T(8,128)(2,1)S(1)} %collective-permute-done.37.refs_1_), channel_id=1, source_target_pairs={{0,4},{2,6},{4,0},{6,2},{8,12},{10,14},{12,8},{14,10},{16,20},{18,... | collective-permute-start | bytes 786440 | tf_op jit(solution)/shard_map/ppermute | solution.py:18
  147.1 9.6 %collective-permute-start.33 = (bf16[4,64,512]{2,1,0:T(8,128)(2,1)S(1)}, bf16[4,64,512]{2,1,0:T(8,128)(2,1)S(1)}, u32[]{:S(2)}, u32[]{:S(2)}) collective-permute-start(bf16[4,64,512]{2,1,0:T(8,128)(2,1)S(1)} %collective-permute-done.32.refs_0_), channel_id=1, source_target_pairs={{0,2},{2,0},{4,6},{6,4},{8,10},{10,8},{12,14},{14,12},{16,18},{18,... | collective-permute-start | bytes 786440 | tf_op jit(solution)/shard_map/ppermute | solution.py:18
  (16 other events, 218.1 us)

commit v2 on v1

--- a/solution.py
+++ b/solution.py
@@ -344,24 +344,27 @@
     )(scalars, residual, mine, other, gain)
 
 
-def feed_chunk(own, other, gate_weight, up_weight, scalars, carry, part, near, far, width, last):
+def feed_chunk(own, other, gate_weight, up_weight, scalars, carry, part, near, far, width, last, staged):
     half = own.shape[1] - STAT_ROWS
     columns = own.shape[2]
-    units = gate_weight.shape[1]
+    units = gate_weight.shape[-1]
     rows = 2 * half
 
     def kernel(s_ref, a_ref, b_ref, gw_hbm, uw_hbm, *rest):
-        g_all, u_all, sems = rest[-3:]
-        rest = rest[:-3]
         copies = []
-        for k in range(far):
-            at = pl.ds(pl.multiple_of((s_ref[0] ^ (k * near + part)) * columns, columns), columns)
-            copies.append(
-                (
-                    pltpu.make_async_copy(gw_hbm.at[at], g_all.at[k], sems.at[k, 0]),
-                    pltpu.make_async_copy(uw_hbm.at[at], u_all.at[k], sems.at[k, 1]),
+        if staged:
+            g_all, u_all = gw_hbm, uw_hbm
+        else:
+            g_all, u_all, sems = rest[-3:]
+            rest = rest[:-3]
+            for k in range(far):
+                at = pl.ds(pl.multiple_of((s_ref[0] ^ (k * near + part)) * columns, columns), columns)
+                copies.append(
+                    (
+                        pltpu.make_async_copy(gw_hbm.at[at], g_all.at[k], sems.at[k, 0]),
+                        pltpu.make_async_copy(uw_hbm.at[at], u_all.at[k], sems.at[k, 1]),
+                    )
                 )
-            )
         for pair in copies:
             for c in pair:
                 c.start()
@@ -389,7 +392,7 @@
             t = jnp.sum(theirs[half:], axis=0, keepdims=True)[:, :LANES]
             top += jnp.where(upper, m, t)
             low += jnp.where(upper, t, m)
-            for c in copies[k]:
+            for c in copies[k] if copies else ():
                 c.wait()
             gate += jnp.dot(lhs, g_all[k], preferred_element_type=f32)
             up += jnp.dot(lhs, u_all[k], preferred_element_type=f32)
@@ -417,10 +420,17 @@
             num_scalar_prefetch=1,
             grid=(1,),
             in_specs=[flat(own.shape), flat(own.shape)]
-            + [pl.BlockSpec(memory_space=pltpu.HBM)] * 2
+            + (
+                [pl.BlockSpec(gate_weight.shape, lambda i, s: (0, 0, 0), pipeline_mode=pl.Buffered(1))]
+                if staged
+                else [pl.BlockSpec(memory_space=pltpu.HBM)]
+            )
+            * 2
             + ([flat(x) for x in acc_shapes] if carry is not None else []),
             out_specs=[flat((half, units))] * 2 if last else [flat(x) for x in acc_shapes],
-            scratch_shapes=[
+            scratch_shapes=[]
+            if staged
+            else [
                 pltpu.VMEM((far, columns, units), bf16),
                 pltpu.VMEM((far, columns, units), bf16),
                 pltpu.SemaphoreType.DMA((far, 2)),
@@ -434,6 +444,36 @@
             flops=4 * rows * far * columns * units, bytes_accessed=4 * far * columns * units, transcendentals=0
         ),
     )(scalars, own, other, gate_weight, up_weight, *(carry or ()))
+
+
+def bring(gate_weight, up_weight, scalars, columns, part, near, far):
+    units = gate_weight.shape[1]
+
+    def kernel(s_ref, gw_hbm, uw_hbm, g_ref, u_ref, sems):
+        copies = []
+        for k in range(far):
+            at = pl.ds(pl.multiple_of((s_ref[0] ^ (k * near + part)) * columns, columns), columns)
+            copies.append(pltpu.make_async_copy(gw_hbm.at[at], g_ref.at[k], sems.at[k, 0]))
+            copies.append(pltpu.make_async_copy(uw_hbm.at[at], u_ref.at[k], sems.at[k, 1]))
+        for c in copies:
+            c.start()
+        for c in copies:
+            c.wait()
+
+    shape = (far, columns, units)
+    return pl.pallas_call(
+        kernel,
+        grid_spec=pltpu.PrefetchScalarGridSpec(
+            num_scalar_prefetch=1,
+            grid=(1,),
+            in_specs=[pl.BlockSpec(memory_space=pltpu.HBM)] * 2,
+            out_specs=[pl.BlockSpec(shape, lambda i, s: (0, 0, 0), pipeline_mode=pl.Buffered(1))] * 2,
+            scratch_shapes=[pltpu.SemaphoreType.DMA((far, 2))],
+        ),
+        out_shape=[jax.ShapeDtypeStruct(shape, bf16)] * 2,
+        compiler_params=pltpu.CompilerParams(vmem_limit_bytes=16 << 20),
+        cost_estimate=pl.CostEstimate(flops=4000000000, bytes_accessed=8 * far * columns * units, transcendentals=0),
+    )(scalars, gate_weight, up_weight)
 
 
 def down_chunk(halves, weight, scalars, carry, part, near, far, last):
@@ -519,8 +559,14 @@
     normed = gather(send, near, far, blocks, stack_join)
     carry = None
     for p in range(near):
+        last = p == near - 1
         other = swap_head(normed[p])
-        carry = feed_chunk(normed[p], other, gate_weight, up_weight, spot, carry, p, near, far, width, p == near - 1)
+        pair = (gate_weight, up_weight)
+        if last:
+            pair = bring(*pair, spot_late, residual.shape[1], p, near, far)
+        carry = feed_chunk(normed[p], other, *pair, spot, carry, p, near, far, width, last, last)
+        if p == 0:
+            spot_late, carry = lax.optimization_barrier((spot, carry))
     hidden = gather_halves(*carry, near, far, blocks, stack_join)
     carry = None
     for p in range(near):

time: 160 us -> 159 us (level)
  waiting for transfers between devices: 55.7 us -> 54.1 us
    pallas_call x0 -> x1, Pallas kernels: none -> 2.76 us  [bring(): pl.pallas_call(kernel, grid_spec=pltpu.PrefetchScalarGridSpec(num_scalar_...]
    pallas_call x4, Pallas kernels: 12.6 us -> 10.8 us  [feed_chunk(): pl.pallas_call(kernel, grid_spec=pltpu.PrefetchScalarGridSpec(num_scalar_...]
    ppermute x36, waiting for transfers between devices: 53.1 us -> 51.4 us  [xor_blk(): return lax.ppermute(x, 'blk', [(i, i ^ mask) for i in range(blocks)])]
  transfers between devices with their start and end apart: 42 -> 42, of which waited for: 20 -> 20; matrix products, arithmetic and copies ran while one was open for 5% -> 5% of each run, Pallas kernels for 24% -> 26%
where the time goes in v2:
time: 159 us; the launch traced here: 158 us
  waiting for transfers between devices  54.1 us (34%)
  starting transfers between devices  48.2 us (30%)
  Pallas kernels  47.2 us (30%)
  local copies, waits for them, and re-layouts  7.6 us (5%)
    ppermute x36, waiting for transfers between devices, xor_blk(): return lax.ppermute(x, 'blk', [(i, i ^ mask) for i in range(blocks)])  51.4 us
    ppermute x36, starting transfers between devices, xor_blk(): return lax.ppermute(x, 'blk', [(i, i ^ mask) for i in range(blocks)])  48 us
    pallas_call x3, Pallas kernels, attention(): pl.pallas_call(kernel, grid_spec=pltpu.PrefetchScalarGridSpec(num_scalar_...  26.6 us
    pallas_call x4, Pallas kernels, feed_chunk(): pl.pallas_call(kernel, grid_spec=pltpu.PrefetchScalarGridSpec(num_scalar_...  10.8 us
    transpose x1, local copies, waits for them, and re-layouts, body(): values = stay(jnp.transpose(value_cache, (0, 2, 1, 3)))  6.62 us
    pallas_call x4, Pallas kernels, down_chunk(): pl.pallas_call(kernel, grid_spec=pltpu.PrefetchScalarGridSpec(num_scalar_...  3.95 us
  transfers between devices with their start and end apart: 42, of which 20 were waited for; matrix products, arithmetic and copies ran while one was open for 5% of the time, Pallas kernels for 26%

profile of v2, /device:TPU:0, one launch (start us, length us, event | category | flops | bytes accessed | tf_op | source)
XLA Modules:
  0.0 158.4 jit_solution(8672608049657392561)
XLA Ops:
  0.0 3.1 %collective-permute-start = (bf16[8,4096]{1,0:T(8,128)(2,1)}, bf16[8,4096]{1,0:T(8,128)(2,1)S(1)}, u32[]{:S(2)}, u32[]{:S(2)}) collective-permute-start(bf16[8,4096]{1,0:T(8,128)(2,1)} %param.10), channel_id=1, source_target_pairs={{0,8},{2,10},{4,12},{6,14},{8,0},{10,2},{12,4},{14,6},{16,24},{18,... | collective-permute-start | bytes 196616 | tf_op jit(solution)/shard_map/ppermute | solution.py:18
  3.1 2.6 %collective-permute-start.1 = (bf16[8,4096]{1,0:T(8,128)(2,1)}, bf16[8,4096]{1,0:T(8,128)(2,1)S(1)}, u32[]{:S(2)}, u32[]{:S(2)}) collective-permute-start(bf16[8,4096]{1,0:T(8,128)(2,1)} %param.10), channel_id=1, source_target_pairs={{0,16},{2,18},{4,20},{6,22},{8,24},{10,26},{12,28},{14,30},{16,0},... | collective-permute-start | bytes 196616 | tf_op jit(solution)/shard_map/ppermute | solution.py:18
  6.6 4.0 %collective-permute-done.1 = bf16[8,4096]{1,0:T(8,128)(2,1)S(1)} collective-permute-done((bf16[8,4096]{1,0:T(8,128)(2,1)}, bf16[8,4096]{1,0:T(8,128)(2,1)S(1)}, u32[]{:S(2)}, u32[]{:S(2)}) %collective-permute-start.1) | collective-permute-done | bytes 65568 | tf_op jit(solution)/shard_map/ppermute | solution.py:18
  15.0 6.6 %copy_bitcast_fusion = (bf16[2,4,2048,128]{3,2,1,0:T(8,128)(2,1)}, bf16[2,4,2048,128]{3,2,1,0:T(8,128)(2,1)}) fusion(bf16[2,2048,4,128]{3,2,1,0:T(4,128)(2,1)} %param.12, bf16[2,2048,4,128]{3,2,1,0:T(4,128)(2,1)} %param.11), kind=kLoop, calls=%fused_computation | loop fusion | bytes 16777216 | tf_op jit(solution)/shard_map/transpose | solution.py:543
  22.2 10.8 %shard_map.101 = (bf16[32,4224]{1,0:T(8,128)(2,1)S(1)}, bf16[32,4224]{1,0:T(8,128)(2,1)S(1)}) custom-call(s32[4]{0:T(128)S(1)} %pad_add_fusion.s_ref, bf16[32,4096]{1,0:T(8,128)(2,1)S(1)} %collective-permute-done.3.refs_0_, bf16[32,4096]{1,0:T(8,128)(2,1)S(1)} %collective-permute-done.4.refs_1_, bf16[2,4,2048,128]{3,2,1,0:T(8,128)(2,1)} %get-tuple-element.52.refs_1_.refs_2_, ...), custom_call_target="tpu_custom_call" | custom-call | flops 4294967296 | bytes 8388608 | tf_op jit(solution)/shard_map/pallas_call | solution.py:200
  34.6 1.7 %collective-permute-start.6 = (bf16[32,4224]{1,0:T(8,128)(2,1)S(1)}, bf16[32,4224]{1,0:T(8,128)(2,1)S(1)}, u32[]{:S(2)}, u32[]{:S(2)}) collective-permute-start(bf16[32,4224]{1,0:T(8,128)(2,1)S(1)} %get-tuple-element.27), channel_id=1, source_target_pairs={{0,4},{2,6},{4,0},{6,2},{8,12},{10,14},{12,8},{14,10},{16,20},{18,... | collective-permute-start | bytes 811016 | tf_op jit(solution)/shard_map/ppermute | solution.py:18
  36.4 7.6 %shard_map.102 = bf16[32,4224]{1,0:T(8,128)(2,1)S(1)} custom-call(s32[4]{0:T(128)S(1)} %pad_add_fusion.s_ref, bf16[32,4096]{1,0:T(8,128)(2,1)S(1)} %collective-permute-done.7.refs_0_, bf16[2,4,2048,128]{3,2,1,0:T(8,128)(2,1)} %get-tuple-element.52.refs_1_.refs_2_, bf16[2,4,2048,128]{3,2,1,0:T(8,128)(2,1)} %get-tuple-element.51.refs_2_.refs_3_), custom_call_target="tpu_custom_call" | custom-call | flops 2147483648 | bytes 8388608 | tf_op jit(solution)/shard_map/pallas_call | solution.py:200
  44.3 8.2 %shard_map.100.refs_0_ = bf16[32,4224]{1,0:T(8,128)(2,1)S(1)} custom-call(s32[4]{0:T(128)S(1)} %pad_add_fusion.s_ref, bf16[32,4096]{1,0:T(8,128)(2,1)S(1)} %constant_dynamic-update-slice_fusion.refs_0_, bf16[2,4,2048,128]{3,2,1,0:T(8,128)(2,1)} %get-tuple-element.52.refs_1_.refs_2_, bf16[2,4,2048,128]{3,2,1,0:T(8,128)(2,1)} %get-tuple-element.51.refs_2_.refs_3_), custom_call_target="tpu_custom_call" | custom-call | flops 2147483648 | bytes 8388608 | tf_op jit(solution)/shard_map/pallas_call | solution.py:200
  53.3 1.8 %collective-permute-start.10 = (bf16[8,4224]{1,0:T(8,128)(2,1)S(1)}, bf16[8,4224]{1,0:T(8,128)(2,1)S(1)}, u32[]{:S(2)}, u32[]{:S(2)}) collective-permute-start(bf16[8,4224]{1,0:T(8,128)(2,1)S(1)} %get-tuple-element.48), channel_id=1, source_target_pairs={{0,16},{2,18},{4,20},{6,22},{8,24},{10,26},{12,28},{14,30},{16,0},... | collective-permute-start | bytes 202760 | tf_op jit(solution)/shard_map/ppermute | solution.py:18
  56.9 2.2 %collective-permute-done.10.refs_2_ = bf16[8,4224]{1,0:T(8,128)(2,1)S(1)} collective-permute-done((bf16[8,4224]{1,0:T(8,128)(2,1)S(1)}, bf16[8,4224]{1,0:T(8,128)(2,1)S(1)}, u32[]{:S(2)}, u32[]{:S(2)}) %collective-permute-start.10) | collective-permute-done | bytes 67616 | tf_op jit(solution)/shard_map/ppermute | solution.py:18
  59.1 2.3 %collective-permute-done.11.refs_3_ = bf16[8,4224]{1,0:T(8,128)(2,1)S(1)} collective-permute-done((bf16[8,4224]{1,0:T(8,128)(2,1)S(1)}, bf16[8,4224]{1,0:T(8,128)(2,1)S(1)}, u32[]{:S(2)}, u32[]{:S(2)}) %collective-permute-start.11) | collective-permute-done | bytes 67616 | tf_op jit(solution)/shard_map/ppermute | solution.py:18
  62.2 2.2 %collective-permute-start.13 = (bf16[8,4096]{1,0:T(8,128)(2,1)S(1)}, bf16[8,4096]{1,0:T(8,128)(2,1)S(1)}, u32[]{:S(2)}, u32[]{:S(2)}) collective-permute-start(bf16[8,4096]{1,0:T(8,128)(2,1)S(1)} %shard_map.104), channel_id=1, source_target_pairs={{0,16},{2,18},{4,20},{6,22},{8,24},{10,26},{12,28},{14,30},{16,0},... | collective-permute-start | bytes 196616 | tf_op jit(solution)/shard_map/ppermute | solution.py:18
  64.5 1.7 %collective-permute-start.14 = (bf16[8,4096]{1,0:T(8,128)(2,1)S(1)}, bf16[8,4096]{1,0:T(8,128)(2,1)S(1)}, u32[]{:S(2)}, u32[]{:S(2)}) collective-permute-start(bf16[8,4096]{1,0:T(8,128)(2,1)S(1)} %shard_map.104), channel_id=1, source_target_pairs={{0,24},{2,26},{4,28},{6,30},{8,16},{10,18},{12,20},{14,22},{16,8},... | collective-permute-start | bytes 196616 | tf_op jit(solution)/shard_map/ppermute | solution.py:18
  67.4 3.1 %collective-permute-done.14 = bf16[8,4096]{1,0:T(8,128)(2,1)S(1)} collective-permute-done((bf16[8,4096]{1,0:T(8,128)(2,1)S(1)}, bf16[8,4096]{1,0:T(8,128)(2,1)S(1)}, u32[]{:S(2)}, u32[]{:S(2)}) %collective-permute-start.14) | collective-permute-done | bytes 65568 | tf_op jit(solution)/shard_map/ppermute | solution.py:18
  74.1 2.9 %collective-permute-done.15.refs_1_ = bf16[32,4096]{1,0:T(8,128)(2,1)S(1)} collective-permute-done((bf16[32,4096]{1,0:T(8,128)(2,1)S(1)}, bf16[32,4096]{1,0:T(8,128)(2,1)S(1)}, u32[]{:S(2)}, u32[]{:S(2)}) %collective-permute-start.15) | collective-permute-done | bytes 262176 | tf_op jit(solution)/shard_map/ppermute | solution.py:18
  77.0 4.1 %collective-permute-done.16.refs_2_ = bf16[32,4096]{1,0:T(8,128)(2,1)S(1)} collective-permute-done((bf16[32,4096]{1,0:T(8,128)(2,1)S(1)}, bf16[32,4096]{1,0:T(8,128)(2,1)S(1)}, u32[]{:S(2)}, u32[]{:S(2)}) %collective-permute-start.16) | collective-permute-done | bytes 262176 | tf_op jit(solution)/shard_map/ppermute | solution.py:18
  81.2 1.7 %out_projection.1.a_ref = bf16[128,512]{1,0:T(8,128)(2,1)S(1)} custom-call(s32[4]{0:T(128)S(1)} %pad_add_fusion.s_ref, bf16[32,4096]{1,0:T(8,128)(2,1)S(1)} %pad_maximum_fusion.1.refs_0_, bf16[32,4096]{1,0:T(8,128)(2,1)S(1)} %collective-permute-done.15.refs_1_, bf16[32,4096]{1,0:T(8,128)(2,1)S(1)} %collective-permute-done.16.refs_2_, ...), custom_call_target="tpu_custom_call" | custom-call | flops 536870912 | bytes 4194304 | tf_op jit(solution)/shard_map/out_projection/pallas_call | solution.py:288
  84.6 2.6 %collective-permute-start.20 = (bf16[72,512]{1,0:T(8,128)(2,1)S(1)}, bf16[72,512]{1,0:T(8,128)(2,1)S(1)}, u32[]{:S(2)}, u32[]{:S(2)}) collective-permute-start(bf16[72,512]{1,0:T(8,128)(2,1)S(1)} %get-tuple-element.29), channel_id=1, source_target_pairs={{0,16},{2,18},{4,20},{6,22},{8,24},{10,26},{12,28},{14,30},{16,0},... | collective-permute-start | bytes 221192 | tf_op jit(solution)/shard_map/ppermute | solution.py:18
  87.2 1.8 %collective-permute-start.21 = (bf16[72,512]{1,0:T(8,128)(2,1)S(1)}, bf16[72,512]{1,0:T(8,128)(2,1)S(1)}, u32[]{:S(2)}, u32[]{:S(2)}) collective-permute-start(bf16[72,512]{1,0:T(8,128)(2,1)S(1)} %get-tuple-element.29), channel_id=1, source_target_pairs={{0,24},{2,26},{4,28},{6,30},{8,16},{10,18},{12,20},{14,22},{16,8},... | collective-permute-start | bytes 221192 | tf_op jit(solution)/shard_map/ppermute | solution.py:18
  90.1 3.4 %collective-permute-done.20 = bf16[72,512]{1,0:T(8,128)(2,1)S(1)} collective-permute-done((bf16[72,512]{1,0:T(8,128)(2,1)S(1)}, bf16[72,512]{1,0:T(8,128)(2,1)S(1)}, u32[]{:S(2)}, u32[]{:S(2)}) %collective-permute-start.20) | collective-permute-done | bytes 73760 | tf_op jit(solution)/shard_map/ppermute | solution.py:18
  97.3 3.1 %shard_map.105 = (f32[128,512]{1,0:T(8,128)S(1)}, f32[128,512]{1,0:T(8,128)S(1)}, f32[8,128]{1,0:T(8,128)S(1)}) custom-call(s32[2]{0:T(128)S(1)} %pad_add_fusion.1.s_ref, bf16[4,72,512]{2,1,0:T(8,128)(2,1)S(1)} %pad_maximum_fusion.a_ref, bf16[4,72,512]{2,1,0:T(8,128)(2,1)S(1)} %collective-permute-done.24.b_ref, bf16[8192,512]{1,0:T(8,128)(2,1)} %gw_hbm.7, ...), custom_call_target="tpu_custom_call" | custom-call | flops 536870912 | bytes 4194304 | tf_op jit(solution)/shard_map/pallas_call | solution.py:417
  100.4 3.2 %collective-permute-done.27.a_ref = bf16[4,72,512]{2,1,0:T(8,128)(2,1)S(1)} collective-permute-done((bf16[4,72,512]{2,1,0:T(8,128)(2,1)S(1)}, bf16[4,72,512]{2,1,0:T(8,128)(2,1)S(1)}, u32[]{:S(2)}, u32[]{:S(2)}) %collective-permute-start.27) | collective-permute-done | bytes 294944 | tf_op jit(solution)/shard_map/ppermute | solution.py:18
  103.6 5.1 %collective-permute-done.25.a_ref = bf16[4,72,512]{2,1,0:T(8,128)(2,1)S(1)} collective-permute-done((bf16[4,72,512]{2,1,0:T(8,128)(2,1)S(1)}, bf16[4,72,512]{2,1,0:T(8,128)(2,1)S(1)}, u32[]{:S(2)}, u32[]{:S(2)}) %collective-permute-start.25) | collective-permute-done | bytes 294944 | tf_op jit(solution)/shard_map/ppermute | solution.py:18
  110.4 2.8 %shard_map.106 = (bf16[4,512,512]{2,1,0:T(8,128)(2,1)S(1)}, bf16[4,512,512]{2,1,0:T(8,128)(2,1)S(1)}) custom-call(s32[2]{0:T(128)S(1)} %pad_add_fusion.1.s_ref, bf16[8192,512]{1,0:T(8,128)(2,1)} %gw_hbm.7, bf16[8192,512]{1,0:T(8,128)(2,1)} %uw_hbm.7), custom_call_target="tpu_custom_call" | custom-call | flops 4000000000 | bytes 8388608 | tf_op jit(solution)/shard_map/pallas_call | solution.py:464
  113.2 3.1 %shard_map.107 = (f32[128,512]{1,0:T(8,128)S(1)}, f32[128,512]{1,0:T(8,128)S(1)}, f32[8,128]{1,0:T(8,128)S(1)}) custom-call(s32[2]{0:T(128)S(1)} %pad_add_fusion.1.s_ref, bf16[4,72,512]{2,1,0:T(8,128)(2,1)S(1)} %collective-permute-done.27.a_ref, bf16[4,72,512]{2,1,0:T(8,128)(2,1)S(1)} %collective-permute-done.28.b_ref, bf16[8192,512]{1,0:T(8,128)(2,1)} %gw_hbm.7, ...), custom_call_target="tpu_custom_call" | custom-call | flops 536870912 | bytes 4194304 | tf_op jit(solution)/shard_map/pallas_call | solution.py:417
  116.3 3.3 %shard_map.108 = (f32[128,512]{1,0:T(8,128)S(1)}, f32[128,512]{1,0:T(8,128)S(1)}, f32[8,128]{1,0:T(8,128)S(1)}) custom-call(s32[2]{0:T(128)S(1)} %pad_add_fusion.1.s_ref, bf16[4,72,512]{2,1,0:T(8,128)(2,1)S(1)} %collective-permute-done.25.a_ref, bf16[4,72,512]{2,1,0:T(8,128)(2,1)S(1)} %collective-permute-done.26.b_ref, bf16[8192,512]{1,0:T(8,128)(2,1)} %gw_hbm.7, ...), custom_call_target="tpu_custom_call" | custom-call | flops 536870912 | bytes 4194304 | tf_op jit(solution)/shard_map/pallas_call | solution.py:417
  120.9 1.7 %collective-permute-start.34 = (bf16[64,512]{1,0:T(8,128)(2,1)S(1)}, bf16[64,512]{1,0:T(8,128)(2,1)S(1)}, u32[]{:S(2)}, u32[]{:S(2)}) collective-permute-start(bf16[64,512]{1,0:T(8,128)(2,1)S(1)} %get-tuple-element.46), channel_id=1, source_target_pairs={{0,8},{2,10},{4,12},{6,14},{8,0},{10,2},{12,4},{14,6},{16,24},{18,... | collective-permute-start | bytes 196616 | tf_op jit(solution)/shard_map/ppermute | solution.py:18
  126.1 2.4 %collective-permute-start.30 = (bf16[64,512]{1,0:T(8,128)(2,1)S(1)}, bf16[64,512]{1,0:T(8,128)(2,1)S(1)}, u32[]{:S(2)}, u32[]{:S(2)}) collective-permute-start(bf16[64,512]{1,0:T(8,128)(2,1)S(1)} %get-tuple-element.45), channel_id=1, source_target_pairs={{0,16},{2,18},{4,20},{6,22},{8,24},{10,26},{12,28},{14,30},{16,0},... | collective-permute-start | bytes 196616 | tf_op jit(solution)/shard_map/ppermute | solution.py:18
  132.8 3.9 %collective-permute-done.30 = bf16[64,512]{1,0:T(8,128)(2,1)S(1)} collective-permute-done((bf16[64,512]{1,0:T(8,128)(2,1)S(1)}, bf16[64,512]{1,0:T(8,128)(2,1)S(1)}, u32[]{:S(2)}, u32[]{:S(2)}) %collective-permute-start.30) | collective-permute-done | bytes 65568 | tf_op jit(solution)/shard_map/ppermute | solution.py:18
  141.3 4.8 %collective-permute-done.32.refs_0_ = bf16[4,64,512]{2,1,0:T(8,128)(2,1)S(1)} collective-permute-done((bf16[4,64,512]{2,1,0:T(8,128)(2,1)S(1)}, bf16[4,64,512]{2,1,0:T(8,128)(2,1)S(1)}, u32[]{:S(2)}, u32[]{:S(2)}) %collective-permute-start.32) | collective-permute-done | bytes 262176 | tf_op jit(solution)/shard_map/ppermute | solution.py:18
  148.9 2.7 %collective-permute-done.39.refs_1_ = bf16[4,64,512]{2,1,0:T(8,128)(2,1)S(1)} collective-permute-done((bf16[4,64,512]{2,1,0:T(8,128)(2,1)S(1)}, bf16[4,64,512]{2,1,0:T(8,128)(2,1)S(1)}, u32[]{:S(2)}, u32[]{:S(2)}) %collective-permute-start.39) | collective-permute-done | bytes 262176 | tf_op jit(solution)/shard_map/ppermute | solution.py:18
  152.7 2.6 %collective-permute-done.38.refs_1_ = bf16[4,64,512]{2,1,0:T(8,128)(2,1)S(1)} collective-permute-done((bf16[4,64,512]{2,1,0:T(8,128)(2,1)S(1)}, bf16[4,64,512]{2,1,0:T(8,128)(2,1)S(1)}, u32[]{:S(2)}, u32[]{:S(2)}) %collective-permute-start.38) | collective-permute-done | bytes 262176 | tf_op jit(solution)/shard_map/ppermute | solution.py:18
  (95 shorter events, 44.7 us)
Async XLA Ops:
  0.0 6.6 %collective-permute-start = (bf16[8,4096]{1,0:T(8,128)(2,1)}, bf16[8,4096]{1,0:T(8,128)(2,1)S(1)}, u32[]{:S(2)}, u32[]{:S(2)}) collective-permute-start(bf16[8,4096]{1,0:T(8,128)(2,1)} %param.10), channel_id=1, source_target_pairs={{0,8},{2,10},{4,12},{6,14},{8,0},{10,2},{12,4},{14,6},{16,24},{18,... | collective-permute-start | bytes 196616 | tf_op jit(solution)/shard_map/ppermute | solution.py:18
  3.1 7.5 %collective-permute-start.1 = (bf16[8,4096]{1,0:T(8,128)(2,1)}, bf16[8,4096]{1,0:T(8,128)(2,1)S(1)}, u32[]{:S(2)}, u32[]{:S(2)}) collective-permute-start(bf16[8,4096]{1,0:T(8,128)(2,1)} %param.10), channel_id=1, source_target_pairs={{0,16},{2,18},{4,20},{6,22},{8,24},{10,26},{12,28},{14,30},{16,0},... | collective-permute-start | bytes 196616 | tf_op jit(solution)/shard_map/ppermute | solution.py:18
  5.6 6.3 %collective-permute-start.2 = (bf16[8,4096]{1,0:T(8,128)(2,1)}, bf16[8,4096]{1,0:T(8,128)(2,1)S(1)}, u32[]{:S(2)}, u32[]{:S(2)}) collective-permute-start(bf16[8,4096]{1,0:T(8,128)(2,1)} %param.10), channel_id=1, source_target_pairs={{0,24},{2,26},{4,28},{6,30},{8,16},{10,18},{12,20},{14,22},{16,8},... | collective-permute-start | bytes 196616 | tf_op jit(solution)/shard_map/ppermute | solution.py:18
  12.0 10.3 %collective-permute-start.3 = (bf16[32,4096]{1,0:T(8,128)(2,1)S(1)}, bf16[32,4096]{1,0:T(8,128)(2,1)S(1)}, u32[]{:S(2)}, u32[]{:S(2)}) collective-permute-start(bf16[32,4096]{1,0:T(8,128)(2,1)S(1)} %constant_dynamic-update-slice_fusion.refs_0_), channel_id=1, source_target_pairs={{0,2},{2,0},{4,6},{6,4},{8,10},{10,8},{12,14},{14,12},{16,18},{18,... | collective-permute-start | bytes 786440 | tf_op jit(solution)/shard_map/ppermute | solution.py:18
  13.5 8.7 %collective-permute-start.4 = (bf16[32,4096]{1,0:T(8,128)(2,1)S(1)}, bf16[32,4096]{1,0:T(8,128)(2,1)S(1)}, u32[]{:S(2)}, u32[]{:S(2)}) collective-permute-start(bf16[32,4096]{1,0:T(8,128)(2,1)S(1)} %constant_dynamic-update-slice_fusion.refs_0_), channel_id=1, source_target_pairs={{0,4},{2,6},{4,0},{6,2},{8,12},{10,14},{12,8},{14,10},{16,20},{18,... | collective-permute-start | bytes 786440 | tf_op jit(solution)/shard_map/ppermute | solution.py:18
  21.7 14.6 %collective-permute-start.7 = (bf16[32,4096]{1,0:T(8,128)(2,1)S(1)}, bf16[32,4096]{1,0:T(8,128)(2,1)S(1)}, u32[]{:S(2)}, u32[]{:S(2)}) collective-permute-start(bf16[32,4096]{1,0:T(8,128)(2,1)S(1)} %constant_dynamic-update-slice_fusion.refs_0_), channel_id=1, source_target_pairs={{0,6},{2,4},{4,2},{6,0},{8,14},{10,12},{12,10},{14,8},{16,22},{18,... | collective-permute-start | bytes 786440 | tf_op jit(solution)/shard_map/ppermute | solution.py:18
  33.1 19.4 %collective-permute-start.5 = (bf16[32,4224]{1,0:T(8,128)(2,1)S(1)}, bf16[32,4224]{1,0:T(8,128)(2,1)S(1)}, u32[]{:S(2)}, u32[]{:S(2)}) collective-permute-start(bf16[32,4224]{1,0:T(8,128)(2,1)S(1)} %get-tuple-element.26), channel_id=1, source_target_pairs={{0,2},{2,0},{4,6},{6,4},{8,10},{10,8},{12,14},{14,12},{16,18},{18,... | collective-permute-start | bytes 811016 | tf_op jit(solution)/shard_map/ppermute | solution.py:18
  34.6 17.9 %collective-permute-start.6 = (bf16[32,4224]{1,0:T(8,128)(2,1)S(1)}, bf16[32,4224]{1,0:T(8,128)(2,1)S(1)}, u32[]{:S(2)}, u32[]{:S(2)}) collective-permute-start(bf16[32,4224]{1,0:T(8,128)(2,1)S(1)} %get-tuple-element.27), channel_id=1, source_target_pairs={{0,4},{2,6},{4,0},{6,2},{8,12},{10,14},{12,8},{14,10},{16,20},{18,... | collective-permute-start | bytes 811016 | tf_op jit(solution)/shard_map/ppermute | solution.py:18
  44.0 8.5 %collective-permute-start.8 = (bf16[32,4224]{1,0:T(8,128)(2,1)S(1)}, bf16[32,4224]{1,0:T(8,128)(2,1)S(1)}, u32[]{:S(2)}, u32[]{:S(2)}) collective-permute-start(bf16[32,4224]{1,0:T(8,128)(2,1)S(1)} %shard_map.102), channel_id=1, source_target_pairs={{0,6},{2,4},{4,2},{6,0},{8,14},{10,12},{12,10},{14,8},{16,22},{18,... | collective-permute-start | bytes 811016 | tf_op jit(solution)/shard_map/ppermute | solution.py:18
  70.6 6.4 %collective-permute-start.15 = (bf16[32,4096]{1,0:T(8,128)(2,1)S(1)}, bf16[32,4096]{1,0:T(8,128)(2,1)S(1)}, u32[]{:S(2)}, u32[]{:S(2)}) collective-permute-start(bf16[32,4096]{1,0:T(8,128)(2,1)S(1)} %pad_maximum_fusion.1.refs_0_), channel_id=1, source_target_pairs={{0,2},{2,0},{4,6},{6,4},{8,10},{10,8},{12,14},{14,12},{16,18},{18,... | collective-permute-start | bytes 786440 | tf_op jit(solution)/shard_map/ppermute | solution.py:18
  72.0 9.2 %collective-permute-start.16 = (bf16[32,4096]{1,0:T(8,128)(2,1)S(1)}, bf16[32,4096]{1,0:T(8,128)(2,1)S(1)}, u32[]{:S(2)}, u32[]{:S(2)}) collective-permute-start(bf16[32,4096]{1,0:T(8,128)(2,1)S(1)} %pad_maximum_fusion.1.refs_0_), channel_id=1, source_target_pairs={{0,4},{2,6},{4,0},{6,2},{8,12},{10,14},{12,8},{14,10},{16,20},{18,... | collective-permute-start | bytes 786440 | tf_op jit(solution)/shard_map/ppermute | solution.py:18
  73.5 7.7 %collective-permute-start.17 = (bf16[32,4096]{1,0:T(8,128)(2,1)S(1)}, bf16[32,4096]{1,0:T(8,128)(2,1)S(1)}, u32[]{:S(2)}, u32[]{:S(2)}) collective-permute-start(bf16[32,4096]{1,0:T(8,128)(2,1)S(1)} %pad_maximum_fusion.1.refs_0_), channel_id=1, source_target_pairs={{0,6},{2,4},{4,2},{6,0},{8,14},{10,12},{12,10},{14,8},{16,22},{18,... | collective-permute-start | bytes 786440 | tf_op jit(solution)/shard_map/ppermute | solution.py:18
  84.6 9.0 %collective-permute-start.20 = (bf16[72,512]{1,0:T(8,128)(2,1)S(1)}, bf16[72,512]{1,0:T(8,128)(2,1)S(1)}, u32[]{:S(2)}, u32[]{:S(2)}) collective-permute-start(bf16[72,512]{1,0:T(8,128)(2,1)S(1)} %get-tuple-element.29), channel_id=1, source_target_pairs={{0,16},{2,18},{4,20},{6,22},{8,24},{10,26},{12,28},{14,30},{16,0},... | collective-permute-start | bytes 221192 | tf_op jit(solution)/shard_map/ppermute | solution.py:18
  87.2 6.4 %collective-permute-start.21 = (bf16[72,512]{1,0:T(8,128)(2,1)S(1)}, bf16[72,512]{1,0:T(8,128)(2,1)S(1)}, u32[]{:S(2)}, u32[]{:S(2)}) collective-permute-start(bf16[72,512]{1,0:T(8,128)(2,1)S(1)} %get-tuple-element.29), channel_id=1, source_target_pairs={{0,24},{2,26},{4,28},{6,30},{8,16},{10,18},{12,20},{14,22},{16,8},... | collective-permute-start | bytes 221192 | tf_op jit(solution)/shard_map/ppermute | solution.py:18
  93.7 9.9 %collective-permute-start.27 = (bf16[4,72,512]{2,1,0:T(8,128)(2,1)S(1)}, bf16[4,72,512]{2,1,0:T(8,128)(2,1)S(1)}, u32[]{:S(2)}, u32[]{:S(2)}) collective-permute-start(bf16[4,72,512]{2,1,0:T(8,128)(2,1)S(1)} %pad_maximum_fusion.a_ref), channel_id=1, source_target_pairs={{0,2},{2,0},{4,6},{6,4},{8,10},{10,8},{12,14},{14,12},{16,18},{18,... | collective-permute-start | bytes 884744 | tf_op jit(solution)/shard_map/ppermute | solution.py:18
  94.7 14.0 %collective-permute-start.25 = (bf16[4,72,512]{2,1,0:T(8,128)(2,1)S(1)}, bf16[4,72,512]{2,1,0:T(8,128)(2,1)S(1)}, u32[]{:S(2)}, u32[]{:S(2)}) collective-permute-start(bf16[4,72,512]{2,1,0:T(8,128)(2,1)S(1)} %pad_maximum_fusion.a_ref), channel_id=1, source_target_pairs={{0,4},{2,6},{4,0},{6,2},{8,12},{10,14},{12,8},{14,10},{16,20},{18,... | collective-permute-start | bytes 884744 | tf_op jit(solution)/shard_map/ppermute | solution.py:18
  95.8 14.6 %collective-permute-start.22 = (bf16[4,72,512]{2,1,0:T(8,128)(2,1)S(1)}, bf16[4,72,512]{2,1,0:T(8,128)(2,1)S(1)}, u32[]{:S(2)}, u32[]{:S(2)}) collective-permute-start(bf16[4,72,512]{2,1,0:T(8,128)(2,1)S(1)} %pad_maximum_fusion.a_ref), channel_id=1, source_target_pairs={{0,6},{2,4},{4,2},{6,0},{8,14},{10,12},{12,10},{14,8},{16,22},{18,... | collective-permute-start | bytes 884744 | tf_op jit(solution)/shard_map/ppermute | solution.py:18
  103.6 9.5 %collective-permute-start.28 = (bf16[4,72,512]{2,1,0:T(8,128)(2,1)S(1)}, bf16[4,72,512]{2,1,0:T(8,128)(2,1)S(1)}, u32[]{:S(2)}, u32[]{:S(2)}) collective-permute-start(bf16[4,72,512]{2,1,0:T(8,128)(2,1)S(1)} %collective-permute-done.27.a_ref), channel_id=1, source_target_pairs={{0,1},{1,0},{2,3},{3,2},{4,5},{5,4},{6,7},{7,6},{8,9},{9,8},{10,11... | collective-permute-start | bytes 884744 | tf_op jit(solution)/shard_map/ppermute | solution.py:23
  108.8 7.5 %collective-permute-start.26 = (bf16[4,72,512]{2,1,0:T(8,128)(2,1)S(1)}, bf16[4,72,512]{2,1,0:T(8,128)(2,1)S(1)}, u32[]{:S(2)}, u32[]{:S(2)}) collective-permute-start(bf16[4,72,512]{2,1,0:T(8,128)(2,1)S(1)} %collective-permute-done.25.a_ref), channel_id=1, source_target_pairs={{0,1},{1,0},{2,3},{3,2},{4,5},{5,4},{6,7},{7,6},{8,9},{9,8},{10,11... | collective-permute-start | bytes 884744 | tf_op jit(solution)/shard_map/ppermute | solution.py:23
  110.4 9.3 %collective-permute-start.23 = (bf16[4,72,512]{2,1,0:T(8,128)(2,1)S(1)}, bf16[4,72,512]{2,1,0:T(8,128)(2,1)S(1)}, u32[]{:S(2)}, u32[]{:S(2)}) collective-permute-start(bf16[4,72,512]{2,1,0:T(8,128)(2,1)S(1)} %collective-permute-done.22.a_ref), channel_id=1, source_target_pairs={{0,1},{1,0},{2,3},{3,2},{4,5},{5,4},{6,7},{7,6},{8,9},{9,8},{10,11... | collective-permute-start | bytes 884744 | tf_op jit(solution)/shard_map/ppermute | solution.py:23
  120.9 7.6 %collective-permute-start.34 = (bf16[64,512]{1,0:T(8,128)(2,1)S(1)}, bf16[64,512]{1,0:T(8,128)(2,1)S(1)}, u32[]{:S(2)}, u32[]{:S(2)}) collective-permute-start(bf16[64,512]{1,0:T(8,128)(2,1)S(1)} %get-tuple-element.46), channel_id=1, source_target_pairs={{0,8},{2,10},{4,12},{6,14},{8,0},{10,2},{12,4},{14,6},{16,24},{18,... | collective-permute-start | bytes 196616 | tf_op jit(solution)/shard_map/ppermute | solution.py:18
  122.6 8.7 %collective-permute-start.35 = (bf16[64,512]{1,0:T(8,128)(2,1)S(1)}, bf16[64,512]{1,0:T(8,128)(2,1)S(1)}, u32[]{:S(2)}, u32[]{:S(2)}) collective-permute-start(bf16[64,512]{1,0:T(8,128)(2,1)S(1)} %get-tuple-element.46), channel_id=1, source_target_pairs={{0,16},{2,18},{4,20},{6,22},{8,24},{10,26},{12,28},{14,30},{16,0},... | collective-permute-start | bytes 196616 | tf_op jit(solution)/shard_map/ppermute | solution.py:18
  124.1 7.2 %collective-permute-start.36 = (bf16[64,512]{1,0:T(8,128)(2,1)S(1)}, bf16[64,512]{1,0:T(8,128)(2,1)S(1)}, u32[]{:S(2)}, u32[]{:S(2)}) collective-permute-start(bf16[64,512]{1,0:T(8,128)(2,1)S(1)} %get-tuple-element.46), channel_id=1, source_target_pairs={{0,24},{2,26},{4,28},{6,30},{8,16},{10,18},{12,20},{14,22},{16,8},... | collective-permute-start | bytes 196616 | tf_op jit(solution)/shard_map/ppermute | solution.py:18
  125.4 7.4 %collective-permute-start.29 = (bf16[64,512]{1,0:T(8,128)(2,1)S(1)}, bf16[64,512]{1,0:T(8,128)(2,1)S(1)}, u32[]{:S(2)}, u32[]{:S(2)}) collective-permute-start(bf16[64,512]{1,0:T(8,128)(2,1)S(1)} %get-tuple-element.45), channel_id=1, source_target_pairs={{0,8},{2,10},{4,12},{6,14},{8,0},{10,2},{12,4},{14,6},{16,24},{18,... | collective-permute-start | bytes 196616 | tf_op jit(solution)/shard_map/ppermute | solution.py:18
  126.1 10.6 %collective-permute-start.30 = (bf16[64,512]{1,0:T(8,128)(2,1)S(1)}, bf16[64,512]{1,0:T(8,128)(2,1)S(1)}, u32[]{:S(2)}, u32[]{:S(2)}) collective-permute-start(bf16[64,512]{1,0:T(8,128)(2,1)S(1)} %get-tuple-element.45), channel_id=1, source_target_pairs={{0,16},{2,18},{4,20},{6,22},{8,24},{10,26},{12,28},{14,30},{16,0},... | collective-permute-start | bytes 196616 | tf_op jit(solution)/shard_map/ppermute | solution.py:18
  128.5 8.3 %collective-permute-start.31 = (bf16[64,512]{1,0:T(8,128)(2,1)S(1)}, bf16[64,512]{1,0:T(8,128)(2,1)S(1)}, u32[]{:S(2)}, u32[]{:S(2)}) collective-permute-start(bf16[64,512]{1,0:T(8,128)(2,1)S(1)} %get-tuple-element.45), channel_id=1, source_target_pairs={{0,24},{2,26},{4,28},{6,30},{8,16},{10,18},{12,20},{14,22},{16,8},... | collective-permute-start | bytes 196616 | tf_op jit(solution)/shard_map/ppermute | solution.py:18
  131.4 8.4 %collective-permute-start.37 = (bf16[4,64,512]{2,1,0:T(8,128)(2,1)S(1)}, bf16[4,64,512]{2,1,0:T(8,128)(2,1)S(1)}, u32[]{:S(2)}, u32[]{:S(2)}) collective-permute-start(bf16[4,64,512]{2,1,0:T(8,128)(2,1)S(1)} %pad_maximum_fusion.3.refs_1_), channel_id=1, source_target_pairs={{0,2},{2,0},{4,6},{6,4},{8,10},{10,8},{12,14},{14,12},{16,18},{18,... | collective-permute-start | bytes 786440 | tf_op jit(solution)/shard_map/ppermute | solution.py:18
  136.8 9.2 %collective-permute-start.32 = (bf16[4,64,512]{2,1,0:T(8,128)(2,1)S(1)}, bf16[4,64,512]{2,1,0:T(8,128)(2,1)S(1)}, u32[]{:S(2)}, u32[]{:S(2)}) collective-permute-start(bf16[4,64,512]{2,1,0:T(8,128)(2,1)S(1)} %pad_maximum_fusion.2.refs_0_), channel_id=1, source_target_pairs={{0,4},{2,6},{4,0},{6,2},{8,12},{10,14},{12,8},{14,10},{16,20},{18,... | collective-permute-start | bytes 786440 | tf_op jit(solution)/shard_map/ppermute | solution.py:18
  137.8 10.1 %collective-permute-start.40 = (bf16[4,64,512]{2,1,0:T(8,128)(2,1)S(1)}, bf16[4,64,512]{2,1,0:T(8,128)(2,1)S(1)}, u32[]{:S(2)}, u32[]{:S(2)}) collective-permute-start(bf16[4,64,512]{2,1,0:T(8,128)(2,1)S(1)} %pad_maximum_fusion.2.refs_0_), channel_id=1, source_target_pairs={{0,2},{2,0},{4,6},{6,4},{8,10},{10,8},{12,14},{14,12},{16,18},{18,... | collective-permute-start | bytes 786440 | tf_op jit(solution)/shard_map/ppermute | solution.py:18
  139.3 12.4 %collective-permute-start.39 = (bf16[4,64,512]{2,1,0:T(8,128)(2,1)S(1)}, bf16[4,64,512]{2,1,0:T(8,128)(2,1)S(1)}, u32[]{:S(2)}, u32[]{:S(2)}) collective-permute-start(bf16[4,64,512]{2,1,0:T(8,128)(2,1)S(1)} %pad_maximum_fusion.3.refs_1_), channel_id=1, source_target_pairs={{0,4},{2,6},{4,0},{6,2},{8,12},{10,14},{12,8},{14,10},{16,20},{18,... | collective-permute-start | bytes 786440 | tf_op jit(solution)/shard_map/ppermute | solution.py:18
  139.8 15.5 %collective-permute-start.38 = (bf16[4,64,512]{2,1,0:T(8,128)(2,1)S(1)}, bf16[4,64,512]{2,1,0:T(8,128)(2,1)S(1)}, u32[]{:S(2)}, u32[]{:S(2)}) collective-permute-start(bf16[4,64,512]{2,1,0:T(8,128)(2,1)S(1)} %collective-permute-done.37.refs_1_), channel_id=1, source_target_pairs={{0,4},{2,6},{4,0},{6,2},{8,12},{10,14},{12,8},{14,10},{16,20},{18,... | collective-permute-start | bytes 786440 | tf_op jit(solution)/shard_map/ppermute | solution.py:18
  146.1 9.2 %collective-permute-start.33 = (bf16[4,64,512]{2,1,0:T(8,128)(2,1)S(1)}, bf16[4,64,512]{2,1,0:T(8,128)(2,1)S(1)}, u32[]{:S(2)}, u32[]{:S(2)}) collective-permute-start(bf16[4,64,512]{2,1,0:T(8,128)(2,1)S(1)} %collective-permute-done.32.refs_0_), channel_id=1, source_target_pairs={{0,2},{2,0},{4,6},{6,4},{8,10},{10,8},{12,14},{14,12},{16,18},{18,... | collective-permute-start | bytes 786440 | tf_op jit(solution)/shard_map/ppermute | solution.py:18
  (16 other events, 215.9 us)
